TPU v7x, 32 devices: a 4x4x1 block of a 4x4x8 slice. The times are simulated.
32 devices in a mesh: dp: 1 (over z), tx: 4 (over y), ty: 8 (over x, core).
Axes of the slice: x: 4, y: 4, z: 1, core: 2. Of those that a mesh axis runs over, the one named last changes fastest.
The devices are a block of a 4x4x8 slice.
Arguments:
- x: bfloat16 [4096, 2048], P('dp', ('tx', 'ty'))
- seg_ids: int32 [4096], P('dp')
- positions: int32 [4096], P('dp')
- ln1_gain: bfloat16 [2, 2048], P(None, ('tx', 'ty'))
- ln1_bias: bfloat16 [2, 2048], P(None, ('tx', 'ty'))
- w_q: bfloat16 [2, 2048, 16, 128], P(None, 'tx', 'ty')
- b_q: bfloat16 [2, 16, 128], P(None, 'ty')
- w_k: bfloat16 [2, 2048, 16, 128], P(None, 'tx', 'ty')
- b_k: bfloat16 [2, 16, 128], P(None, 'ty')
- w_v: bfloat16 [2, 2048, 16, 128], P(None, 'tx', 'ty')
- b_v: bfloat16 [2, 16, 128], P(None, 'ty')
- w_o: bfloat16 [2, 16, 128, 2048], P(None, 'ty', None, 'tx')
- b_o: bfloat16 [2, 2048], P(None, ('tx', 'ty'))
- ln2_gain: bfloat16 [2, 2048], P(None, ('tx', 'ty'))
- ln2_bias: bfloat16 [2, 2048], P(None, ('tx', 'ty'))
- w_up: bfloat16 [2, 2048, 8192], P(None, 'tx', 'ty')
- b_up: bfloat16 [2, 8192], P(None, ('ty', 'tx'))
- w_down: bfloat16 [2, 8192, 2048], P(None, 'ty', 'tx')
- b_down: bfloat16 [2, 2048], P(None, ('tx', 'ty'))
Outputs:
- output 1: bfloat16 [4096, 2048], P('dp', ('tx', 'ty'))
- output 2: bfloat16 [2, 4096, 16, 128], P(None, ('dp', 'tx'), 'ty')
- output 3: bfloat16 [2, 4096, 16, 128], P(None, ('dp', 'tx'), 'ty')
All inputs are finite; a program needn't handle non-finite values.
Results may differ from a plain program's by a relative error of at most 0.0119909.
Values are sent between devices in bfloat16 or wider.
A program may use at most 768 MiB of HBM per device.

v0:
```python
import math
import functools
import jax
import jax.numpy as jnp
from jax import lax
from jax.experimental import pallas as pl
from jax.experimental.pallas import tpu as pltpu
from jax.sharding import PartitionSpec as P

MESH = pl.DeviceIdType.MESH
F32 = jnp.float32
BF16 = jnp.bfloat16
ROPE_THETA = 100000.0
LOG2E = 1.4426950408889634
LANES = 128
BK = 1024


def rows_norm(x_f32, gain, bias):
    width = x_f32.shape[-1]
    mean = jnp.sum(x_f32, axis=-1, keepdims=True) / width
    var = jnp.sum(x_f32 * x_f32, axis=-1, keepdims=True) / width - mean * mean
    normed = (x_f32 - mean) * lax.rsqrt(var + 1e-5)
    return (normed * gain + bias).astype(BF16)


def gelu_tanh(x):
    return 0.5 * x * (1.0 + jnp.tanh(0.7978845608028654 * (x + 0.044715 * (x * x * x))))


def rows(at, n):
    return pl.ds(pl.multiple_of(at, n), n)


class Place:
    def __init__(self, num_tx, num_ty):
        self.num_tx, self.num_ty, self.n_chip = num_tx, num_ty, num_ty // 2
        self.y = lax.axis_index('tx')
        self.ty = lax.axis_index('ty')
        self.x = self.ty // 2
        self.c = lax.rem(self.ty, 2)
        self.me = self.y * num_ty + self.ty
        self.sib = self.at(self.y, self.x * 2 + 1 - self.c)
        self.right, self.left = self.beside(1), self.beside(self.n_chip - 1)
        self.above, self.below = self.over(1), self.over(num_tx - 1)

    def at(self, y, ty):
        return {'tx': y, 'ty': ty}

    def chip(self, k):
        return lax.rem(self.x + k, self.n_chip)

    def side(self, k):
        return lax.rem(self.y + k, self.num_tx)

    def beside(self, k):
        return self.at(self.y, self.chip(k) * 2 + self.c)

    def over(self, k):
        return self.at(self.side(k), self.ty)


def remote(src, dst, send_sem, recv_sem, to):
    return pltpu.make_async_remote_copy(src_ref=src, dst_ref=dst, send_sem=send_sem, recv_sem=recv_sem, device_id=to,
                                        device_id_type=MESH)


def copy_or_send(here, src, dst, send_sem, recv_sem, to):
    @pl.when(here)
    def _():
        pltpu.make_async_copy(src, dst, recv_sem).start()

    @pl.when(jnp.logical_not(here))
    def _():
        remote(src, dst, send_sem, recv_sem, to).start()


def took(ref, sem):
    pltpu.make_async_copy(ref, ref, sem).wait()


class RingGather:
    SEMS = 14

    def __init__(self, p, view, sems):
        self.p = p
        self.view = view
        self.sems = sems
        x, c, d = p.x, p.c, 1 - p.c
        far, left, right = p.chip(2), p.chip(p.n_chip - 1), p.chip(1)
        self.plan = [(x, 0, p.right, left), (x, 1, p.left, right), (x, 1, p.right, left), (x, 0, p.left, right),
                     (left, 0, p.right, far), (right, 1, p.left, far),
                     (x, 0, p.sib, x), (x, 1, p.sib, x), (left, 0, p.sib, left), (left, 1, p.sib, left),
                     (right, 0, p.sib, right), (right, 1, p.sib, right), (far, 0, p.sib, far), (far, 1, p.sib, far)]

    def out(self, i):
        chip, half, to, _ = self.plan[i]
        ref = self.view(chip, self.p.c, half)
        return remote(ref, ref, self.sems.at[0, i], self.sems.at[1, i], to)

    def arrived(self, i):
        _, half, to, chip = self.plan[i]
        core = self.p.c if i < 6 else 1 - self.p.c
        ref = self.view(chip, core, half)
        remote(ref, ref, self.sems.at[0, i], self.sems.at[1, i], to).wait_recv()

    def start(self):
        for i in (6, 7, 0, 1, 2, 3):
            self.out(i).start()

    def own(self):
        self.arrived(6)
        self.arrived(7)

    def relay(self):
        self.arrived(0)
        self.out(4).start()
        self.arrived(1)
        self.out(5).start()
        self.out(8).start()
        self.out(11).start()

    def near(self):
        self.arrived(2)
        self.out(9).start()
        self.arrived(3)
        self.out(10).start()

    def near_right(self):
        self.arrived(10)
        self.arrived(11)

    def near_left(self):
        self.arrived(8)
        self.arrived(9)

    def far(self):
        self.arrived(4)
        self.out(12).start()
        self.arrived(5)
        self.out(13).start()

    def far_done(self):
        self.arrived(12)
        self.arrived(13)

    def drain(self):
        for i in range(self.SEMS):
            self.out(i).wait_send()


class ColumnGather:
    SEMS = 8

    def __init__(self, p, pieces, sems):
        self.p = p
        self.pieces = pieces
        self.sems = sems

    def copy(self, n, i):
        p = self.p
        src, dst = self.pieces[n]
        up, down = p.side(1), p.side(p.num_tx - 1)
        half, to = ((0, p.above), (1, p.below), (1, p.above), (0, p.below), (0, p.above), (1, p.below))[i]
        here = src(half) if i < 4 else dst(down if i == 4 else up, half)
        there = dst((p.y, p.y, p.y, p.y, down, up)[i], half)
        return remote(here, there, self.sems.at[0, n * self.SEMS + i], self.sems.at[1, n * self.SEMS + i], to)

    def arrived(self, n, i):
        p = self.p
        src, dst = self.pieces[n]
        up, down, far = p.side(1), p.side(p.num_tx - 1), p.side(2)
        half, frm = ((0, down), (1, up), (1, down), (0, up), (0, far), (1, far))[i]
        remote(src(half), dst(frm, half), self.sems.at[0, n * self.SEMS + i], self.sems.at[1, n * self.SEMS + i],
               p.above).wait_recv()

    def own(self, n, half):
        src, dst = self.pieces[n]
        return pltpu.make_async_copy(src(half), dst(self.p.y, half), self.sems.at[1, n * self.SEMS + 6 + half])

    def start_first(self):
        for i in (0, 1):
            for n in range(len(self.pieces)):
                self.copy(n, i).start()

    def start_second(self):
        for i in (2, 3):
            for n in range(len(self.pieces)):
                self.copy(n, i).start()
        for n in range(len(self.pieces)):
            self.own(n, 0).start()
            self.own(n, 1).start()

    def start(self):
        self.start_first()
        self.start_second()

    def relay(self):
        for n in range(len(self.pieces)):
            self.arrived(n, 0)
            self.copy(n, 4).start()
            self.arrived(n, 1)
            self.copy(n, 5).start()

    def shard(self, k):
        for n in range(len(self.pieces)):
            if k == 0:
                self.own(n, 0).wait()
                self.own(n, 1).wait()
            elif k == 2:
                self.arrived(n, 4)
                self.arrived(n, 5)
            else:
                self.arrived(n, 3 if k == 1 else 2)

    def finish(self):
        for k in (0, 1, 3, 2):
            self.shard(k)

    def drain(self):
        for n in range(len(self.pieces)):
            for i in range(6):
                self.copy(n, i).wait_send()


S_DIRECT_R, S_DIRECT_L, S_FAR_R, S_FAR_L, S_SUM_R, S_SUM_L = range(6)


def decoder_kernel(num_tx, num_ty, n_layers,
                   xt_hbm, g1_ref, b1_ref, g2_ref, b2_ref, bo_ref, bd_ref, bup_ref, bq_ref, bk_ref, bv_ref, pos_ref,
                   wq_hbm, wk_hbm, wv_hbm, wo_hbm, wu_hbm, wd_hbm,
                   yt_hbm, kc_hbm, vc_hbm, go_hbm,
                   xt, vrow, vloc, vbuf, vec, bloc, bup, raw, ws, w, wu, wd, wo, cs, a_all, hid, st, cst, kv, vt, qh, ob, obuf,
                   g, full, sibin, far_in, fin,
                   x_sems, v_sems, b_sems, y_sems, a_sems, u_sems, wq_sems, wo_sems, wx_sems, wu_sems, wd_sems,
                   kv_sems, o_sems, p_sems, r_sems, l_sems, c_sems):
    p = Place(num_tx, num_ty)
    n_dev = num_tx * num_ty
    n_chip, x, y, c, ty = p.n_chip, p.x, p.y, p.c, p.ty
    n_row, width = hid.shape
    blk = 2 * n_row
    half_row = n_row // 2
    loc_heads, head_w = wq_hbm.shape[2], wq_hbm.shape[3]
    loc_w = loc_heads * head_w
    col_w = wd.shape[3]
    piece_w = xt_hbm.shape[0]
    last = n_chip - 1
    mine, other = rows(c * n_row, n_row), rows((1 - c) * n_row, n_row)

    barrier = pltpu.get_barrier_semaphore()
    ids = [lax.rem(p.me + k, n_dev) for k in range(1, n_dev)]
    devs = [p.at(d // num_ty, lax.rem(d, num_ty)) for d in ids]
    for to in devs:
        pl.semaphore_signal(barrier, inc=1, device_id=to, device_id_type=MESH)

    def load_raw(l):
        return [pltpu.make_async_copy(src.at[l], raw.at[i], l_sems.at[i]) for i, src in enumerate((wq_hbm, wk_hbm, wv_hbm))]

    def flatten(l):
        for i, ld in enumerate(load_raw(l)):
            ld.wait()
            ws[l, i] = raw[i].reshape(ws.shape[2], loc_w)
    for ld in load_raw(0):
        ld.start()
    vrow[...] = jnp.zeros_like(vrow)
    for i, ref in enumerate((g1_ref, b1_ref, g2_ref, b2_ref, bo_ref, bd_ref)):
        vrow[i * n_layers:(i + 1) * n_layers, :piece_w] = ref[...].astype(F32)
    vloc[...] = vrow[...].astype(BF16)
    bloc[...] = jnp.zeros_like(bloc)
    bloc[:n_layers, :] = bup_ref[...].astype(F32)
    flatten(0)
    pl.semaphore_wait(barrier, n_dev - 1)

    def halves(ref, l, n):
        return lambda h: ref.at[l, pl.ds(h * n, n)]

    def shard_rows(dst, l, n_shard, n, cols):
        return lambda ys, h: dst.at[l, rows(ys * n_shard + h * n, n), cols]

    qkv_rows = ws.shape[2]
    up_rows = wu_hbm.shape[1]
    down_rows = wd_hbm.shape[1]
    o_rows = wo_hbm.shape[1]

    def gather_qkv(l):
        n = qkv_rows // 2
        return ColumnGather(p, [((lambda h, i=i: ws.at[l, i, pl.ds(h * n, n)]),
                                 shard_rows(w, l, qkv_rows, n, pl.ds(i * loc_w, loc_w))) for i in range(3)], wq_sems)

    def gather_up(l):
        n = up_rows // 2
        return ColumnGather(p, [(halves(wu_hbm, l, n), shard_rows(wu, l, up_rows, n, slice(None)))], wu_sems)

    def gather_down(l):
        n = down_rows // 2
        return ColumnGather(p, [(halves(wd_hbm, l, n), lambda ys, h: wd.at[l, ys, pl.ds(h * n, n)])], wd_sems)

    def gather_o(l):
        n = o_rows // 2
        return ColumnGather(p, [(halves(wo_hbm, l, n), lambda ys, h: go_hbm.at[l, ys, rows(ty * o_rows + h * n, n)])], wo_sems)

    def spread_o(l):
        n = num_tx // 2
        return RingGather(p, lambda chip, core, h: go_hbm.at[l, pl.ds(h * n, n), rows((chip * 2 + core) * o_rows, o_rows)],
                          wx_sems)

    g_qkv = [gather_qkv(l) for l in range(n_layers)]
    g_up = [gather_up(l) for l in range(n_layers)]
    g_down = [gather_down(l) for l in range(n_layers)]
    g_o = [gather_o(l) for l in range(n_layers)]
    s_o = [spread_o(l) for l in range(n_layers)]

    for d, to in zip(ids, devs):
        remote(xt_hbm.at[:, rows(d * n_row, n_row)], xt.at[rows(p.me * piece_w, piece_w)], x_sems.at[0], x_sems.at[1], to).start()
        remote(vloc, vbuf.at[p.me], v_sems.at[0], v_sems.at[1], to).start()
    g_qkv[0].start()
    pltpu.make_async_copy(xt_hbm.at[:, rows(p.me * n_row, n_row)], xt.at[rows(p.me * piece_w, piece_w)], x_sems.at[1]).start()
    pltpu.make_async_copy(vloc, vbuf.at[p.me], v_sems.at[1]).start()
    bup_w = bup_ref.shape[1]
    for k in range(1, num_tx):
        remote(bloc, bup.at[:, rows(y * bup_w, bup_w)], b_sems.at[0], b_sems.at[1], p.over(k)).start()
    pltpu.make_async_copy(bloc, bup.at[:, rows(y * bup_w, bup_w)], b_sems.at[1]).start()
    for l in range(1, n_layers):
        for ld in load_raw(l):
            ld.start()
        flatten(l)

    lane = lax.broadcasted_iota(jnp.int32, (1, head_w), 1)
    inv_freq = jnp.exp(lax.rem(lane, head_w // 2).astype(F32) * (-2.0 * math.log(ROPE_THETA) / head_w))
    sign = jnp.where(lane < head_w // 2, -1.0, 1.0)

    def angles(k, carry):
        pos = pos_ref[pl.ds(y * n_chip + k, 1), :].astype(F32)
        ang = jnp.broadcast_to(pos, (head_w, blk)).T * inv_freq
        cs[0, rows(k * blk, blk), :] = jnp.cos(ang)
        cs[1, rows(k * blk, blk), :] = jnp.sin(ang) * sign
        return carry
    lax.fori_loop(0, n_chip, angles, 0)
    took(vbuf, v_sems.at[1])
    per = LANES // piece_w
    for j in range(width // LANES):
        vec[:, j * LANES:(j + 1) * LANES] = jnp.concatenate(
            [vbuf[per * j + i][:, :piece_w].astype(F32) for i in range(per)], axis=1)
    took(xt, x_sems.at[1])

    def turn(j, carry):
        hid[:, rows(j * LANES, LANES)] = xt[rows(j * LANES, LANES), :].T
        return carry
    lax.fori_loop(0, width // LANES, turn, 0)

    def vector(i, l):
        return vec[i * n_layers + l:i * n_layers + l + 1, :]

    def row_gather(sems):
        return RingGather(p, lambda chip, core, h: a_all.at[chip, rows(core * n_row + h * half_row, half_row)], sems)

    def order(n):
        return n + n // 2 - 2 * (n // 3)

    def each(n_from, n_to, body, hooks):
        def step(n, carry):
            for at_n, hook in hooks.items():
                @pl.when(n == at_n)
                def _():
                    for h in hook:
                        h()
            body(order(n))
            return carry
        lax.fori_loop(n_from, n_to, step, 0)

    def project(l, k):
        slot = p.chip(k)
        at_row = rows(slot * blk, blk)
        acc = jnp.dot(a_all[slot], w[l], preferred_element_type=F32)
        cos_t, sin_t = cs[0, at_row, :], cs[1, at_row, :]
        for i, bias in enumerate((bq_ref, bk_ref, bv_ref)):
            parts = []
            for h in range(loc_heads):
                lo = i * loc_w + h * head_w
                v = acc[:, lo:lo + head_w] + bias[l, h:h + 1, :].astype(F32)
                if i < 2:
                    v = v * cos_t + pltpu.roll(v, head_w // 2, 1) * sin_t
                parts.append(v.astype(BF16))
                st[k, h, i] = parts[-1]
            if i > 0:
                cst[k, i - 1] = jnp.concatenate(parts, axis=1).reshape(blk, loc_heads, head_w)
        at_tok = rows((y * n_chip + slot) * blk, blk)
        par = lax.rem(slot, 2)
        at_q = rows((y * (n_chip // 2) + slot // 2) * blk, blk)
        for h in range(loc_heads):
            yd = c * loc_heads + h
            for r in range(2):
                copy_or_send(jnp.logical_and(yd == y, c == r), st.at[k, h, 1 + r], kv.at[r, at_tok], kv_sems.at[0],
                             kv_sems.at[1], p.at(yd, x * 2 + r))
            copy_or_send(jnp.logical_and(yd == y, c == par), st.at[k, h, 0], qh.at[at_q], kv_sems.at[2], kv_sems.at[3],
                         p.at(yd, x * 2 + par))
        pltpu.make_async_copy(cst.at[k, 0], kc_hbm.at[l, at_row], c_sems.at[0]).start()
        pltpu.make_async_copy(cst.at[k, 1], vc_hbm.at[l, at_row], c_sems.at[1]).start()

    n_q = ob.shape[0]
    q_grp = 2 * blk
    n_grp = n_q * blk // q_grp
    n_sub = BK // blk

    def attend(hooks):
        def step(n, carry):
            grp = n_grp - 1 - n
            q = qh[rows(grp * q_grp, q_grp), :]
            q_col = lax.broadcasted_iota(jnp.int32, (1, blk), 1)
            at_q = [(2 * (2 * grp + i) + c) for i in range(2)]
            q_pos = jnp.concatenate([q_col + b * blk for b in at_q], axis=1)
            first = q_pos - jnp.concatenate([pos_ref[pl.ds(b, 1), :] for b in at_q], axis=1)
            key = lax.broadcasted_iota(jnp.int32, (blk, q_grp), 0)

            def score(j, m, diag):
                s = lax.dot_general(kv[0, rows(j * BK, BK), :], q, (((1,), (1,)), ((), ())),
                                    preferred_element_type=F32) * head_w ** -0.5
                for i in range(n_sub):
                    k_pos = key + (j * BK + i * blk)
                    ok = k_pos >= first
                    if diag:
                        ok = jnp.logical_and(ok, k_pos <= q_pos)
                    part = jnp.where(ok, s[i * blk:(i + 1) * blk], -1e30)
                    full[j, :, i * q_grp:(i + 1) * q_grp] = part
                    m = jnp.maximum(m, jnp.max(part.reshape(blk // 8, 8, q_grp), axis=0))
                return m
            m = lax.fori_loop(0, grp, lambda j, m: score(j, m, False), jnp.full((8, q_grp), -1e30, F32))
            m = jnp.max(score(grp, m, True), axis=0, keepdims=True)

            def expo(j, t):
                for i in range(n_sub):
                    e = jnp.exp(full[j, :, i * q_grp:(i + 1) * q_grp] - m)
                    full[j, :, i * q_grp:(i + 1) * q_grp] = e
                    t = t + jnp.sum(e.reshape(blk // 8, 8, q_grp), axis=0)
                return t
            t = lax.fori_loop(0, grp + 1, expo, jnp.zeros((8, q_grp), F32))
            inv = 1.0 / jnp.sum(t, axis=0, keepdims=True)

            def apply(j, acc):
                prob = jnp.concatenate([(full[j, :, i * q_grp:(i + 1) * q_grp] * inv).astype(BF16) for i in range(n_sub)], axis=0)
                return acc + jnp.dot(vt[:, rows(j * BK, BK)], prob, preferred_element_type=F32)
            out = lax.fori_loop(0, grp + 1, apply, jnp.zeros((head_w, q_grp), F32)).T.astype(BF16)
            cols_o = rows((x * num_tx + y) * head_w, head_w)
            for i, b in enumerate(at_q):
                ob[2 * grp + i] = out[i * blk:(i + 1) * blk]
                yt, xd = b // n_chip, lax.rem(b, n_chip)
                for r in range(2):
                    here = jnp.logical_and(jnp.logical_and(yt == y, xd == x), c == r)
                    copy_or_send(here, ob.at[2 * grp + i, pl.ds(r * n_row, n_row)], obuf.at[:, cols_o], o_sems.at[0],
                                 o_sems.at[1], p.at(yt, xd * 2 + r))
            for at_n, hook in hooks.items():
                @pl.when(n == at_n)
                def _():
                    for h in hook:
                        h()
            return carry
        lax.fori_loop(0, n_grp, step, 0)

    def up(l, k):
        slot = p.chip(k)

        def part(n, carry):
            cc = rows(n * 512, 512)
            h = jnp.dot(a_all[slot], wu[l, :, cc], preferred_element_type=F32) + bup[l:l + 1, cc]
            g[k, :, cc] = gelu_tanh(h).astype(BF16)
            return carry
        lax.fori_loop(0, wu.shape[2] // 512, part, 0)

    blocks = (0, 1, last, 2)
    cols = [rows(p.side(k) * col_w, col_w) for k in blocks]
    top, bottom = rows(c * n_row, half_row), rows(c * n_row + half_row, half_row)

    def to_sibling(k, j):
        i = k * num_tx + j
        return remote(full.at[k, other, cols[j]], sibin.at[k, :, cols[j]], p_sems.at[0, i], p_sems.at[1, i], p.sib)

    def rs(kind, j):
        k, part, dst, to = ((1, bottom, fin.at[0], p.right), (last, top, fin.at[1], p.left), (2, top, far_in.at[0], p.right),
                            (2, bottom, far_in.at[1], p.left), (1, top, fin.at[2], p.right),
                            (last, bottom, fin.at[3], p.left))[kind]
        i = kind * num_tx + j
        return remote(full.at[k, part, cols[j]], dst.at[:, cols[j]], r_sems.at[0, i], r_sems.at[1, i], to)

    def partials(l, j):
        def part(n, carry):
            k = order(lax.rem(n + 1, n_chip))
            full[k, :, cols[j]] = jnp.dot(g[k], wd[l, p.side(blocks[j])], preferred_element_type=F32)
            to_sibling(k, j).start()
            return carry
        lax.fori_loop(0, n_chip, part, 0)

    def pair_sum(k, j):
        to_sibling(k, j).wait_recv()
        full[k, mine, cols[j]] = full[k, mine, cols[j]] + sibin[k, :, cols[j]]

    def send_partials(j):
        pair_sum(1, j)
        rs(S_DIRECT_R, j).start()
        pair_sum(last, j)
        rs(S_DIRECT_L, j).start()
        pair_sum(2, j)
        rs(S_FAR_R, j).start()
        rs(S_FAR_L, j).start()
        pair_sum(0, j)

    def pass_on(j):
        rs(S_FAR_R, j).wait_recv()
        full[1, top, cols[j]] = full[1, top, cols[j]] + far_in[0, :, cols[j]]
        rs(S_SUM_R, j).start()
        rs(S_FAR_L, j).wait_recv()
        full[last, bottom, cols[j]] = full[last, bottom, cols[j]] + far_in[1, :, cols[j]]
        rs(S_SUM_L, j).start()

    def complete(l, j):
        cc = cols[j]
        bias = vec[5 * n_layers + l:5 * n_layers + l + 1, cc]
        for kind in (S_DIRECT_R, S_DIRECT_L, S_SUM_R, S_SUM_L):
            rs(kind, j).wait_recv()
        for part, out, ins in ((top, pl.ds(0, half_row), (1, 2)), (bottom, pl.ds(half_row, half_row), (0, 3))):
            tot = full[0, part, cc] + fin[ins[0], :, cc] + fin[ins[1], :, cc]
            hid[out, cc] = (hid[out, cc].astype(F32) + tot + bias).astype(BF16)

    def give_back(j):
        row = p.side(blocks[j])

        def turn_back(n, carry):
            at_c = rows(row * col_w + n * LANES, LANES)
            xt[at_c, :] = hid[:, at_c].T
            return carry
        lax.fori_loop(0, col_w // LANES, turn_back, 0)
        for k in range(num_ty):
            to_ty = lax.rem(ty + k, num_ty)
            copy_or_send(jnp.logical_and(row == y, k == 0), xt.at[rows((row * num_ty + to_ty) * piece_w, piece_w)],
                         yt_hbm.at[:, rows(p.me * n_row, n_row)], y_sems.at[0], y_sems.at[1], p.at(row, to_ty))

    for l in range(n_layers):
        first_layer, last_layer = l == 0, l == n_layers - 1
        a_all[x, mine, :] = rows_norm(hid[...].astype(F32), vector(0, l), vector(1, l))
        ga = row_gather(a_sems)
        ga.start()
        if first_layer:
            g_qkv[l].relay()
            g_o[l].start()
            ga.relay()
            ga.own()
            ga.near()
            ga.near_right()
            ga.near_left()
            ga.far()
            ga.far_done()
            ga.drain()
            g_qkv[l].finish()
            each(0, n_chip, lambda k: project(l, k), {1: [g_o[l].relay]})
        else:
            ga.relay()
            ga.own()
            g_qkv[l].finish()
            each(0, last, lambda k: project(l, k), {1: [ga.near, ga.near_right, ga.near_left, g_o[l].relay]})
            ga.far()
            ga.far_done()
            ga.drain()
            project(l, 2)
        g_up[l].start_first()
        g_o[l].finish()
        s_o[l].start()
        role = kv.at[c]
        took(role, kv_sems.at[1])
        forward = remote(role, role, kv_sems.at[4], kv_sems.at[5], p.sib)
        forward.start()
        s_o[l].relay()
        took(qh, kv_sems.at[3])
        remote(kv.at[1 - c], kv.at[1 - c], kv_sems.at[4], kv_sems.at[5], p.sib).wait_recv()
        forward.wait_send()

        def turn_v(n, carry):
            vt[:, rows(n * LANES, LANES)] = kv[1, rows(n * LANES, LANES), :].T
            return carry
        lax.fori_loop(0, vt.shape[1] // LANES, turn_v, 0)
        attend({1: [s_o[l].near]})
        g_up[l].start_second()
        g_up[l].relay()
        g_down[l].start()
        s_o[l].far()
        s_o[l].own()
        s_o[l].near_right()
        s_o[l].near_left()
        s_o[l].far_done()
        n_step = wo.shape[2]
        per_col = col_w // n_step

        def load_o(t):
            return pltpu.make_async_copy(go_hbm.at[l, t // per_col, :, rows(lax.rem(t, per_col) * n_step, n_step)],
                                         wo.at[lax.rem(t, 2)], l_sems.at[lax.rem(t, 2)])
        load_o(0).start()
        load_o(1).start()
        took(obuf, o_sems.at[1])

        def out_product(t, carry):
            load_o(t).wait()
            cc = rows(t * n_step, n_step)
            bias = vec[4 * n_layers + l:4 * n_layers + l + 1, cc]
            hid[:, cc] = (hid[:, cc].astype(F32) + jnp.dot(obuf[...], wo[lax.rem(t, 2)], preferred_element_type=F32)
                          + bias).astype(BF16)

            @pl.when(t + 2 < width // n_step)
            def _():
                load_o(t + 2).start()
            return carry
        lax.fori_loop(0, width // n_step, out_product, 0)
        a_all[x, mine, :] = rows_norm(hid[...].astype(F32), vector(2, l), vector(3, l))
        gu = row_gather(u_sems)
        gu.start()
        if first_layer:
            took(bup, b_sems.at[1])
        gu.own()
        gu.relay()
        g_up[l].finish()
        each(0, n_chip, lambda k: up(l, k), {1: [gu.near, gu.near_right, gu.near_left], last: [gu.far, gu.far_done]})
        gu.drain()
        g_down[l].relay()
        if not last_layer:
            g_qkv[l].drain()
            g_o[l].drain()
            g_qkv[l + 1].start()
        for j in range(num_tx):
            if j == num_tx - 1:
                pass_on(j - 1)
            g_down[l].shard(blocks[j])
            partials(l, j)
            send_partials(j)
            if 0 < j < num_tx - 1:
                pass_on(j - 1)
            if j > 1:
                complete(l, j - 2)
                if last_layer:
                    give_back(j - 2)
        if not last_layer:
            g_qkv[l + 1].relay()
            g_o[l + 1].start()
        pass_on(num_tx - 1)
        for j in range(num_tx - 2, num_tx):
            complete(l, j)
            if last_layer:
                give_back(j)
        for j in range(num_tx):
            for k in range(n_chip):
                to_sibling(k, j).wait_send()
            for kind in range(6):
                rs(kind, j).wait_send()
        s_o[l].drain()
        g_up[l].drain()
        g_down[l].drain()
        if last_layer:
            g_qkv[l].drain()
            g_o[l].drain()
        sent_away(p, kv, qh, kv_sems, loc_heads)
        o_away(p, obuf, o_sems, head_w)
        took(kc_hbm.at[l], c_sems.at[0])
        took(vc_hbm.at[l], c_sems.at[1])

    took(xt_hbm.at[:, pl.ds(0, (n_dev - 1) * n_row)], x_sems.at[0])
    took(vbuf.at[pl.ds(0, n_dev - 1)], v_sems.at[0])
    took(bup.at[:, pl.ds(0, (num_tx - 1) * bup_w)], b_sems.at[0])
    took(yt_hbm, y_sems.at[1])
    took(xt.at[pl.ds(0, (n_dev - 1) * piece_w)], y_sems.at[0])


def sent_away(p, kv, qh, kv_sems, loc_heads):
    stays = p.c == p.y // loc_heads
    n_tok = kv.shape[1]
    n_q = qh.shape[0]

    @pl.when(stays)
    def _():
        took(kv.at[0, pl.ds(0, n_tok * 3 // 4)], kv_sems.at[0])
        took(qh.at[pl.ds(0, n_q * 3 // 4)], kv_sems.at[2])

    @pl.when(jnp.logical_not(stays))
    def _():
        took(kv.at[0], kv_sems.at[0])
        took(qh, kv_sems.at[2])


def o_away(p, obuf, o_sems, head_w):
    stays = lax.rem(p.x, 2) == p.c

    @pl.when(stays)
    def _():
        took(obuf.at[:, pl.ds(0, obuf.shape[1] - head_w)], o_sems.at[0])

    @pl.when(jnp.logical_not(stays))
    def _():
        took(obuf, o_sems.at[0])


def decoder(num_tx, num_ty, xt, vectors, b_up, b_qkv, pos, wq, wk, wv, wo, wu, wd):
    n_layers, d_rows, loc_heads, head_w = wq.shape
    n_dev = num_tx * num_ty
    n_chip = num_ty // 2
    piece_w, n_tok = xt.shape
    width = piece_w * n_dev
    n_row = n_tok // n_dev
    blk = 2 * n_row
    loc_w = loc_heads * head_w
    tok_loc = n_tok // num_tx
    ff = wu.shape[2]
    col_w = wd.shape[2]
    n_q = n_tok // (2 * blk)
    n_vec = -(-len(vectors) * n_layers // 16) * 16
    vm = pl.BlockSpec(memory_space=pltpu.VMEM)
    hb = pl.BlockSpec(memory_space=pl.ANY)
    V = pltpu.VMEM
    dma = pltpu.SemaphoreType.DMA
    cache = jax.ShapeDtypeStruct((n_layers, tok_loc, loc_heads, head_w), BF16)
    go = jax.ShapeDtypeStruct((n_layers, num_tx, wo.shape[1] * num_ty, col_w), BF16)
    CG, RG = ColumnGather.SEMS, RingGather.SEMS
    return pl.pallas_call(
        functools.partial(decoder_kernel, num_tx, num_ty, n_layers),
        out_shape=(jax.ShapeDtypeStruct((piece_w, n_tok), BF16), cache, cache, go),
        in_specs=[hb] + [vm] * 11 + [hb] * 6,
        out_specs=(hb,) * 4,
        scratch_shapes=[V((width, n_row), BF16), V((n_vec, LANES), F32), V((n_vec, LANES), BF16), V((n_dev, n_vec, LANES), BF16),
                        V((n_vec, width), F32), V((8, b_up.shape[1]), F32), V((8, ff), F32),
                        V((3, d_rows, loc_heads, head_w), BF16), V((n_layers, 3, d_rows, loc_w), BF16),
                        V((n_layers, width, 3 * loc_w), BF16), V((n_layers, width, ff), BF16),
                        V((n_layers, num_tx, ff, col_w), BF16), V((2, width, col_w // 2), BF16),
                        V((2, tok_loc, head_w), F32),
                        V((n_chip, blk, width), BF16), V((n_row, width), BF16),
                        V((n_chip, loc_heads, 3, blk, head_w), BF16), V((n_chip, 2, blk, loc_heads, head_w), BF16),
                        V((2, n_tok, head_w), BF16), V((head_w, n_tok), BF16), V((n_q * blk, head_w), BF16),
                        V((n_q, blk, head_w), BF16), V((n_row, width), BF16), V((n_chip, blk, ff), BF16),
                        V((n_chip, blk, width), F32), V((n_chip, n_row, width), F32),
                        V((2, n_row // 2, width), F32), V((4, n_row // 2, width), F32),
                        dma((2,)), dma((2,)), dma((2,)), dma((2,)), dma((2, RG)), dma((2, RG)), dma((2, 3 * CG)), dma((2, CG)),
                        dma((2, RG)), dma((2, CG)), dma((2, CG)), dma((6,)), dma((2,)), dma((2, n_chip * num_tx)),
                        dma((2, 6 * num_tx)), dma((3,)), dma((2,))],
        compiler_params=pltpu.CompilerParams(collective_id=1, has_side_effects=True, vmem_limit_bytes=63 << 20),
        name="decoder",
    )(xt, *vectors, b_up, *b_qkv, pos, wq, wk, wv, wo, wu, wd)[:3]


def solution(mesh):
    num_tx = mesh.shape['tx']
    num_ty = mesh.shape['ty']
    width_spec = P('dp', ('tx', 'ty'))
    vec_spec = P(None, ('tx', 'ty'))
    proj_spec = P(None, 'tx', 'ty', None)
    head_spec = P(None, 'ty', None)
    cache_spec = P(None, ('dp', 'tx'), 'ty', None)
    in_specs = (width_spec, P('dp'), P('dp'), vec_spec, vec_spec, proj_spec, head_spec, proj_spec, head_spec,
                proj_spec, head_spec, P(None, 'ty', None, 'tx'), vec_spec, vec_spec, vec_spec,
                P(None, 'tx', 'ty'), P(None, ('ty', 'tx')), P(None, 'ty', 'tx'), vec_spec)
    out_specs = (width_spec, cache_spec, cache_spec)

    def device_fn(x_loc, seg_all, pos_all, ln1_gain, ln1_bias, w_q, b_q, w_k, b_k, w_v, b_v, w_o, b_o,
                  ln2_gain, ln2_bias, w_up, b_up, w_down, b_down):
        n_tok = x_loc.shape[0]
        blk = 2 * n_tok // (num_tx * num_ty)
        yt, k, v = decoder(num_tx, num_ty, x_loc.T, (ln1_gain, ln1_bias, ln2_gain, ln2_bias, b_o, b_down), b_up,
                           (b_q, b_k, b_v), pos_all.reshape(-1, blk), w_q, w_k, w_v,
                           w_o.reshape(w_o.shape[0], -1, w_o.shape[-1]), w_up, w_down)
        return yt.T, k, v

    return jax.shard_map(device_fn, mesh=mesh, in_specs=in_specs, out_specs=out_specs, check_vma=False)
```

profile of v0, /device:TPU:97, one launch (start us, length us, event | category | flops | bytes accessed | tf_op | source)
XLA Modules:
  0.0 335.0 jit_solution(16875872223433151445)
XLA Ops:
  0.6 1.3 reshape.12.pos_ref
  2.0 327.2 %decoder.1 = (bf16[64,4096]{1,0:T(8,128)(2,1)}, bf16[2,1024,2,128]{3,2,1,0:T(2,128)(2,1)}, bf16[2,1024,2,128]{3,2,1,0:T(2,128)(2,1)}, bf16[2,4,2048,512]{3,2,1,0:T(8,128)(2,1)}) custom-call(bf16[64,4096]{1,0:T(8,128)(2,1)} %bitcast.3, bf16[2,64]{1,0:T(2,128)(2,1)} %g1_ref.1, bf16[2,64]{1,0:T(2,128)(2,1)} %b1_ref.1, bf16[2,64]{1,0:T(2,128)(2,1)} %g2_ref.1, ...), custom_call_target="tpu_custom_call" | custom-call | tf_op jit(solution)/shard_map/decoder/pallas_call | solution.py:717
  329.2 0.0 copy-start
  329.2 2.0 copy.24
  331.1 2.9 copy.25
  334.1 0.0 copy-done
  334.1 1.0 copy.26
Async XLA Ops:
  329.2 4.9 %copy-start = (bf16[2,1024,2,128]{3,2,1,0:T(2,128)(2,1)S(1)}, bf16[2,1024,2,128]{3,2,1,0:T(2,128)(2,1)}, u32[]{:S(2)}) copy-start(bf16[2,1024,2,128]{3,2,1,0:T(2,128)(2,1)} %get-tuple-element.14) | copy-start | bytes 3145732
where the time goes:
time: 336 us; the launch traced here: 335 us
  Pallas kernels  327 us (97%)
  local copies, waits for them, and re-layouts  7.17 us (2%)
    pallas_call x1, Pallas kernels, decoder(): pl.pallas_call(functools.partial(decoder_kernel, num_tx, num_ty, n_layers...  327 us

commit v1 on v0

--- a/solution.py
+++ b/solution.py
@@ -152,10 +152,11 @@
 class ColumnGather:
     SEMS = 8
 
-    def __init__(self, p, pieces, sems):
+    def __init__(self, p, pieces, sems, early=0):
         self.p = p
         self.pieces = pieces
         self.sems = sems
+        self.early = early
 
     def copy(self, n, i):
         p = self.p
@@ -182,12 +183,16 @@
         for i in (0, 1):
             for n in range(len(self.pieces)):
                 self.copy(n, i).start()
+        self.rest(range(self.early))
 
     def start_second(self):
+        self.rest(range(self.early, len(self.pieces)))
+
+    def rest(self, which):
         for i in (2, 3):
-            for n in range(len(self.pieces)):
+            for n in which:
                 self.copy(n, i).start()
-        for n in range(len(self.pieces)):
+        for n in which:
             self.own(n, 0).start()
             self.own(n, 1).start()
 
@@ -229,11 +234,11 @@
 def decoder_kernel(num_tx, num_ty, n_layers,
                    xt_hbm, g1_ref, b1_ref, g2_ref, b2_ref, bo_ref, bd_ref, bup_ref, bq_ref, bk_ref, bv_ref, pos_ref,
                    wq_hbm, wk_hbm, wv_hbm, wo_hbm, wu_hbm, wd_hbm,
-                   yt_hbm, kc_hbm, vc_hbm, go_hbm,
-                   xt, vrow, vloc, vbuf, vec, bloc, bup, raw, ws, w, wu, wd, wo, cs, a_all, hid, st, cst, kv, vt, qh, ob, obuf,
+                   yt_ref, kc_ref, vc_ref,
+                   xt, vrow, vloc, vbuf, vec, bloc, bup, raw, ws, w, wu, wd, wo, cs, a_all, hid, st, sv, kt, vt, qh, ob, obuf,
                    g, full, sibin, far_in, fin,
                    x_sems, v_sems, b_sems, y_sems, a_sems, u_sems, wq_sems, wo_sems, wx_sems, wu_sems, wd_sems,
-                   kv_sems, o_sems, p_sems, r_sems, l_sems, c_sems):
+                   kv_sems, o_sems, p_sems, r_sems, l_sems):
     p = Place(num_tx, num_ty)
     n_dev = num_tx * num_ty
     n_chip, x, y, c, ty = p.n_chip, p.x, p.y, p.c, p.ty
@@ -242,7 +247,7 @@
     half_row = n_row // 2
     loc_heads, head_w = wq_hbm.shape[2], wq_hbm.shape[3]
     loc_w = loc_heads * head_w
-    col_w = wd.shape[3]
+    col_w = wd.shape[2]
     piece_w = xt_hbm.shape[0]
     last = n_chip - 1
     mine, other = rows(c * n_row, n_row), rows((1 - c) * n_row, n_row)
@@ -274,8 +279,8 @@
     def halves(ref, l, n):
         return lambda h: ref.at[l, pl.ds(h * n, n)]
 
-    def shard_rows(dst, l, n_shard, n, cols):
-        return lambda ys, h: dst.at[l, rows(ys * n_shard + h * n, n), cols]
+    def shard_rows(dst, n_shard, n, at_cols):
+        return lambda ys, h: dst.at[rows(ys * n_shard + h * n, n), at_cols]
 
     qkv_rows = ws.shape[2]
     up_rows = wu_hbm.shape[1]
@@ -285,24 +290,24 @@
     def gather_qkv(l):
         n = qkv_rows // 2
         return ColumnGather(p, [((lambda h, i=i: ws.at[l, i, pl.ds(h * n, n)]),
-                                 shard_rows(w, l, qkv_rows, n, pl.ds(i * loc_w, loc_w))) for i in range(3)], wq_sems)
+                                 shard_rows(w, qkv_rows, n, pl.ds(i * loc_w, loc_w))) for i in range(3)], wq_sems)
 
     def gather_up(l):
-        n = up_rows // 2
-        return ColumnGather(p, [(halves(wu_hbm, l, n), shard_rows(wu, l, up_rows, n, slice(None)))], wu_sems)
+        n, half = up_rows // 2, wu.shape[1] // 2
+        return ColumnGather(p, [((lambda h, at_c=at_c: wu_hbm.at[l, pl.ds(h * n, n), at_c]), shard_rows(wu, up_rows, n, at_c))
+                                for at_c in (pl.ds(0, half), pl.ds(half, half))], wu_sems, early=1)
 
     def gather_down(l):
         n = down_rows // 2
-        return ColumnGather(p, [(halves(wd_hbm, l, n), lambda ys, h: wd.at[l, ys, pl.ds(h * n, n)])], wd_sems)
+        return ColumnGather(p, [(halves(wd_hbm, l, n), lambda ys, h: wd.at[ys, pl.ds(h * n, n)])], wd_sems)
 
     def gather_o(l):
         n = o_rows // 2
-        return ColumnGather(p, [(halves(wo_hbm, l, n), lambda ys, h: go_hbm.at[l, ys, rows(ty * o_rows + h * n, n)])], wo_sems)
+        return ColumnGather(p, [(halves(wo_hbm, l, n), lambda ys, h: wo.at[ys, rows(ty * o_rows + h * n, n)])], wo_sems)
 
     def spread_o(l):
         n = num_tx // 2
-        return RingGather(p, lambda chip, core, h: go_hbm.at[l, pl.ds(h * n, n), rows((chip * 2 + core) * o_rows, o_rows)],
-                          wx_sems)
+        return RingGather(p, lambda chip, core, h: wo.at[pl.ds(h * n, n), rows((chip * 2 + core) * o_rows, o_rows)], wx_sems)
 
     g_qkv = [gather_qkv(l) for l in range(n_layers)]
     g_up = [gather_up(l) for l in range(n_layers)]
@@ -313,7 +318,8 @@
     for d, to in zip(ids, devs):
         remote(xt_hbm.at[:, rows(d * n_row, n_row)], xt.at[rows(p.me * piece_w, piece_w)], x_sems.at[0], x_sems.at[1], to).start()
         remote(vloc, vbuf.at[p.me], v_sems.at[0], v_sems.at[1], to).start()
-    g_qkv[0].start()
+    g_o[0].start()
+    g_qkv[0].start_first()
     pltpu.make_async_copy(xt_hbm.at[:, rows(p.me * n_row, n_row)], xt.at[rows(p.me * piece_w, piece_w)], x_sems.at[1]).start()
     pltpu.make_async_copy(vloc, vbuf.at[p.me], v_sems.at[1]).start()
     bup_w = bup_ref.shape[1]
@@ -371,7 +377,7 @@
     def project(l, k):
         slot = p.chip(k)
         at_row = rows(slot * blk, blk)
-        acc = jnp.dot(a_all[slot], w[l], preferred_element_type=F32)
+        acc = jnp.dot(a_all[slot], w[...], preferred_element_type=F32)
         cos_t, sin_t = cs[0, at_row, :], cs[1, at_row, :]
         for i, bias in enumerate((bq_ref, bk_ref, bv_ref)):
             parts = []
@@ -380,22 +386,23 @@
                 v = acc[:, lo:lo + head_w] + bias[l, h:h + 1, :].astype(F32)
                 if i < 2:
                     v = v * cos_t + pltpu.roll(v, head_w // 2, 1) * sin_t
-                parts.append(v.astype(BF16))
-                st[k, h, i] = parts[-1]
+                v = v.astype(BF16)
+                parts.append(v)
+                if i < 2:
+                    st[k, h, i] = v
+                else:
+                    sv[k, h] = v.T
             if i > 0:
-                cst[k, i - 1] = jnp.concatenate(parts, axis=1).reshape(blk, loc_heads, head_w)
+                (kc_ref, vc_ref)[i - 1][l, at_row] = jnp.concatenate(parts, axis=1).reshape(blk, loc_heads, head_w)
         at_tok = rows((y * n_chip + slot) * blk, blk)
         par = lax.rem(slot, 2)
         at_q = rows((y * (n_chip // 2) + slot // 2) * blk, blk)
         for h in range(loc_heads):
             yd = c * loc_heads + h
-            for r in range(2):
-                copy_or_send(jnp.logical_and(yd == y, c == r), st.at[k, h, 1 + r], kv.at[r, at_tok], kv_sems.at[0],
-                             kv_sems.at[1], p.at(yd, x * 2 + r))
+            for r, (src, dst) in enumerate(((st.at[k, h, 1], kt.at[at_tok]), (sv.at[k, h], vt.at[:, at_tok]))):
+                copy_or_send(jnp.logical_and(yd == y, c == r), src, dst, kv_sems.at[0], kv_sems.at[1], p.at(yd, x * 2 + r))
             copy_or_send(jnp.logical_and(yd == y, c == par), st.at[k, h, 0], qh.at[at_q], kv_sems.at[2], kv_sems.at[3],
                          p.at(yd, x * 2 + par))
-        pltpu.make_async_copy(cst.at[k, 0], kc_hbm.at[l, at_row], c_sems.at[0]).start()
-        pltpu.make_async_copy(cst.at[k, 1], vc_hbm.at[l, at_row], c_sems.at[1]).start()
 
     n_q = ob.shape[0]
     q_grp = 2 * blk
@@ -411,10 +418,10 @@
             q_pos = jnp.concatenate([q_col + b * blk for b in at_q], axis=1)
             first = q_pos - jnp.concatenate([pos_ref[pl.ds(b, 1), :] for b in at_q], axis=1)
             key = lax.broadcasted_iota(jnp.int32, (blk, q_grp), 0)
+            scale = head_w ** -0.5 * LOG2E
 
             def score(j, m, diag):
-                s = lax.dot_general(kv[0, rows(j * BK, BK), :], q, (((1,), (1,)), ((), ())),
-                                    preferred_element_type=F32) * head_w ** -0.5
+                s = lax.dot_general(kt[rows(j * BK, BK), :], q, (((1,), (1,)), ((), ())), preferred_element_type=F32)
                 for i in range(n_sub):
                     k_pos = key + (j * BK + i * blk)
                     ok = k_pos >= first
@@ -429,7 +436,7 @@
 
             def expo(j, t):
                 for i in range(n_sub):
-                    e = jnp.exp(full[j, :, i * q_grp:(i + 1) * q_grp] - m)
+                    e = jnp.exp2((full[j, :, i * q_grp:(i + 1) * q_grp] - m) * scale)
                     full[j, :, i * q_grp:(i + 1) * q_grp] = e
                     t = t + jnp.sum(e.reshape(blk // 8, 8, q_grp), axis=0)
                 return t
@@ -461,10 +468,10 @@
 
         def part(n, carry):
             cc = rows(n * 512, 512)
-            h = jnp.dot(a_all[slot], wu[l, :, cc], preferred_element_type=F32) + bup[l:l + 1, cc]
+            h = jnp.dot(a_all[slot], wu[:, cc], preferred_element_type=F32) + bup[l:l + 1, cc]
             g[k, :, cc] = gelu_tanh(h).astype(BF16)
             return carry
-        lax.fori_loop(0, wu.shape[2] // 512, part, 0)
+        lax.fori_loop(0, wu.shape[1] // 512, part, 0)
 
     blocks = (0, 1, last, 2)
     cols = [rows(p.side(k) * col_w, col_w) for k in blocks]
@@ -481,10 +488,10 @@
         i = kind * num_tx + j
         return remote(full.at[k, part, cols[j]], dst.at[:, cols[j]], r_sems.at[0, i], r_sems.at[1, i], to)
 
-    def partials(l, j):
+    def partials(j):
         def part(n, carry):
             k = order(lax.rem(n + 1, n_chip))
-            full[k, :, cols[j]] = jnp.dot(g[k], wd[l, p.side(blocks[j])], preferred_element_type=F32)
+            full[k, :, cols[j]] = jnp.dot(g[k], wd[p.side(blocks[j])], preferred_element_type=F32)
             to_sibling(k, j).start()
             return carry
         lax.fori_loop(0, n_chip, part, 0)
@@ -531,7 +538,16 @@
         for k in range(num_ty):
             to_ty = lax.rem(ty + k, num_ty)
             copy_or_send(jnp.logical_and(row == y, k == 0), xt.at[rows((row * num_ty + to_ty) * piece_w, piece_w)],
-                         yt_hbm.at[:, rows(p.me * n_row, n_row)], y_sems.at[0], y_sems.at[1], p.at(row, to_ty))
+                         yt_ref.at[:, rows(p.me * n_row, n_row)], y_sems.at[0], y_sems.at[1], p.at(row, to_ty))
+
+    def start_forward():
+        @pl.when(c == 0)
+        def _():
+            remote(kt, kt, kv_sems.at[4], kv_sems.at[5], p.sib).start()
+
+        @pl.when(c != 0)
+        def _():
+            remote(vt, vt, kv_sems.at[4], kv_sems.at[5], p.sib).start()
 
     for l in range(n_layers):
         first_layer, last_layer = l == 0, l == n_layers - 1
@@ -539,74 +555,58 @@
         ga = row_gather(a_sems)
         ga.start()
         if first_layer:
+            g_o[l].relay()
+            g_qkv[l].start_second()
+            ga.relay()
             g_qkv[l].relay()
-            g_o[l].start()
-            ga.relay()
             ga.own()
             ga.near()
+            g_o[l].finish()
+            s_o[l].start()
             ga.near_right()
             ga.near_left()
             ga.far()
             ga.far_done()
             ga.drain()
             g_qkv[l].finish()
-            each(0, n_chip, lambda k: project(l, k), {1: [g_o[l].relay]})
+            each(0, n_chip, lambda k: project(l, k), {})
         else:
+            g_qkv[l].relay()
             ga.relay()
             ga.own()
+            g_o[l].finish()
+            s_o[l].start()
             g_qkv[l].finish()
-            each(0, last, lambda k: project(l, k), {1: [ga.near, ga.near_right, ga.near_left, g_o[l].relay]})
+            each(0, last, lambda k: project(l, k), {1: [ga.near, ga.near_right, ga.near_left]})
             ga.far()
             ga.far_done()
             ga.drain()
             project(l, 2)
         g_up[l].start_first()
-        g_o[l].finish()
-        s_o[l].start()
-        role = kv.at[c]
-        took(role, kv_sems.at[1])
-        forward = remote(role, role, kv_sems.at[4], kv_sems.at[5], p.sib)
-        forward.start()
         s_o[l].relay()
+        took(kt, kv_sems.at[1])
+        start_forward()
         took(qh, kv_sems.at[3])
-        remote(kv.at[1 - c], kv.at[1 - c], kv_sems.at[4], kv_sems.at[5], p.sib).wait_recv()
-        forward.wait_send()
-
-        def turn_v(n, carry):
-            vt[:, rows(n * LANES, LANES)] = kv[1, rows(n * LANES, LANES), :].T
-            return carry
-        lax.fori_loop(0, vt.shape[1] // LANES, turn_v, 0)
-        attend({1: [s_o[l].near]})
+        took(kt, kv_sems.at[5])
+        took(kt, kv_sems.at[4])
+        attend({0: [s_o[l].near]})
         g_up[l].start_second()
         g_up[l].relay()
+        g_qkv[l].drain()
         g_down[l].start()
         s_o[l].far()
         s_o[l].own()
         s_o[l].near_right()
         s_o[l].near_left()
         s_o[l].far_done()
-        n_step = wo.shape[2]
-        per_col = col_w // n_step
-
-        def load_o(t):
-            return pltpu.make_async_copy(go_hbm.at[l, t // per_col, :, rows(lax.rem(t, per_col) * n_step, n_step)],
-                                         wo.at[lax.rem(t, 2)], l_sems.at[lax.rem(t, 2)])
-        load_o(0).start()
-        load_o(1).start()
         took(obuf, o_sems.at[1])
 
         def out_product(t, carry):
-            load_o(t).wait()
-            cc = rows(t * n_step, n_step)
+            cc = rows(t * col_w, col_w)
             bias = vec[4 * n_layers + l:4 * n_layers + l + 1, cc]
-            hid[:, cc] = (hid[:, cc].astype(F32) + jnp.dot(obuf[...], wo[lax.rem(t, 2)], preferred_element_type=F32)
-                          + bias).astype(BF16)
-
-            @pl.when(t + 2 < width // n_step)
-            def _():
-                load_o(t + 2).start()
+            hid[:, cc] = (hid[:, cc].astype(F32) + jnp.dot(obuf[...], wo[t], preferred_element_type=F32) + bias).astype(BF16)
             return carry
-        lax.fori_loop(0, width // n_step, out_product, 0)
+        lax.fori_loop(0, num_tx, out_product, 0)
         a_all[x, mine, :] = rows_norm(hid[...].astype(F32), vector(2, l), vector(3, l))
         gu = row_gather(u_sems)
         gu.start()
@@ -617,26 +617,27 @@
         g_up[l].finish()
         each(0, n_chip, lambda k: up(l, k), {1: [gu.near, gu.near_right, gu.near_left], last: [gu.far, gu.far_done]})
         gu.drain()
+        s_o[l].drain()
+        g_o[l].drain()
+        g_up[l].drain()
         g_down[l].relay()
         if not last_layer:
-            g_qkv[l].drain()
-            g_o[l].drain()
-            g_qkv[l + 1].start()
+            g_qkv[l + 1].start_first()
         for j in range(num_tx):
-            if j == num_tx - 1:
-                pass_on(j - 1)
             g_down[l].shard(blocks[j])
-            partials(l, j)
+            if j == num_tx - 1 and not last_layer:
+                g_o[l + 1].start()
+            partials(j)
             send_partials(j)
-            if 0 < j < num_tx - 1:
+            if j > 0:
                 pass_on(j - 1)
             if j > 1:
                 complete(l, j - 2)
                 if last_layer:
                     give_back(j - 2)
         if not last_layer:
-            g_qkv[l + 1].relay()
-            g_o[l + 1].start()
+            g_o[l + 1].relay()
+            g_qkv[l + 1].start_second()
         pass_on(num_tx - 1)
         for j in range(num_tx - 2, num_tx):
             complete(l, j)
@@ -647,37 +648,30 @@
                 to_sibling(k, j).wait_send()
             for kind in range(6):
                 rs(kind, j).wait_send()
-        s_o[l].drain()
-        g_up[l].drain()
         g_down[l].drain()
-        if last_layer:
-            g_qkv[l].drain()
-            g_o[l].drain()
-        sent_away(p, kv, qh, kv_sems, loc_heads)
+        sent_away(p, kt, qh, kv_sems, loc_heads)
         o_away(p, obuf, o_sems, head_w)
-        took(kc_hbm.at[l], c_sems.at[0])
-        took(vc_hbm.at[l], c_sems.at[1])
 
     took(xt_hbm.at[:, pl.ds(0, (n_dev - 1) * n_row)], x_sems.at[0])
     took(vbuf.at[pl.ds(0, n_dev - 1)], v_sems.at[0])
     took(bup.at[:, pl.ds(0, (num_tx - 1) * bup_w)], b_sems.at[0])
-    took(yt_hbm, y_sems.at[1])
+    took(yt_ref, y_sems.at[1])
     took(xt.at[pl.ds(0, (n_dev - 1) * piece_w)], y_sems.at[0])
 
 
-def sent_away(p, kv, qh, kv_sems, loc_heads):
+def sent_away(p, kt, qh, kv_sems, loc_heads):
     stays = p.c == p.y // loc_heads
-    n_tok = kv.shape[1]
+    n_tok = kt.shape[0]
     n_q = qh.shape[0]
 
     @pl.when(stays)
     def _():
-        took(kv.at[0, pl.ds(0, n_tok * 3 // 4)], kv_sems.at[0])
+        took(kt.at[pl.ds(0, n_tok * 3 // 4)], kv_sems.at[0])
         took(qh.at[pl.ds(0, n_q * 3 // 4)], kv_sems.at[2])
 
     @pl.when(jnp.logical_not(stays))
     def _():
-        took(kv.at[0], kv_sems.at[0])
+        took(kt, kv_sems.at[0])
         took(qh, kv_sems.at[2])
 
 
@@ -712,31 +706,29 @@
     V = pltpu.VMEM
     dma = pltpu.SemaphoreType.DMA
     cache = jax.ShapeDtypeStruct((n_layers, tok_loc, loc_heads, head_w), BF16)
-    go = jax.ShapeDtypeStruct((n_layers, num_tx, wo.shape[1] * num_ty, col_w), BF16)
     CG, RG = ColumnGather.SEMS, RingGather.SEMS
     return pl.pallas_call(
         functools.partial(decoder_kernel, num_tx, num_ty, n_layers),
-        out_shape=(jax.ShapeDtypeStruct((piece_w, n_tok), BF16), cache, cache, go),
+        out_shape=(jax.ShapeDtypeStruct((piece_w, n_tok), BF16), cache, cache),
         in_specs=[hb] + [vm] * 11 + [hb] * 6,
-        out_specs=(hb,) * 4,
+        out_specs=(vm,) * 3,
         scratch_shapes=[V((width, n_row), BF16), V((n_vec, LANES), F32), V((n_vec, LANES), BF16), V((n_dev, n_vec, LANES), BF16),
                         V((n_vec, width), F32), V((8, b_up.shape[1]), F32), V((8, ff), F32),
                         V((3, d_rows, loc_heads, head_w), BF16), V((n_layers, 3, d_rows, loc_w), BF16),
-                        V((n_layers, width, 3 * loc_w), BF16), V((n_layers, width, ff), BF16),
-                        V((n_layers, num_tx, ff, col_w), BF16), V((2, width, col_w // 2), BF16),
-                        V((2, tok_loc, head_w), F32),
+                        V((width, 3 * loc_w), BF16), V((width, ff), BF16), V((num_tx, ff, col_w), BF16),
+                        V((num_tx, width, col_w), BF16), V((2, tok_loc, head_w), F32),
                         V((n_chip, blk, width), BF16), V((n_row, width), BF16),
-                        V((n_chip, loc_heads, 3, blk, head_w), BF16), V((n_chip, 2, blk, loc_heads, head_w), BF16),
-                        V((2, n_tok, head_w), BF16), V((head_w, n_tok), BF16), V((n_q * blk, head_w), BF16),
+                        V((n_chip, loc_heads, 2, blk, head_w), BF16), V((n_chip, loc_heads, head_w, blk), BF16),
+                        V((n_tok, head_w), BF16), V((head_w, n_tok), BF16), V((n_q * blk, head_w), BF16),
                         V((n_q, blk, head_w), BF16), V((n_row, width), BF16), V((n_chip, blk, ff), BF16),
                         V((n_chip, blk, width), F32), V((n_chip, n_row, width), F32),
                         V((2, n_row // 2, width), F32), V((4, n_row // 2, width), F32),
                         dma((2,)), dma((2,)), dma((2,)), dma((2,)), dma((2, RG)), dma((2, RG)), dma((2, 3 * CG)), dma((2, CG)),
-                        dma((2, RG)), dma((2, CG)), dma((2, CG)), dma((6,)), dma((2,)), dma((2, n_chip * num_tx)),
-                        dma((2, 6 * num_tx)), dma((3,)), dma((2,))],
+                        dma((2, RG)), dma((2, 2 * CG)), dma((2, CG)), dma((6,)), dma((2,)), dma((2, n_chip * num_tx)),
+                        dma((2, 6 * num_tx)), dma((3,))],
         compiler_params=pltpu.CompilerParams(collective_id=1, has_side_effects=True, vmem_limit_bytes=63 << 20),
         name="decoder",
-    )(xt, *vectors, b_up, *b_qkv, pos, wq, wk, wv, wo, wu, wd)[:3]
+    )(xt, *vectors, b_up, *b_qkv, pos, wq, wk, wv, wo, wu, wd)
 
 
 def solution(mesh):

time: 336 us -> 319 us (0.949)
  Pallas kernels: 327 us -> 311 us
    pallas_call x1, Pallas kernels: 327 us -> 311 us  [decoder(): pl.pallas_call(functools.partial(decoder_kernel, num_tx, num_ty, n_layers...]
where the time goes in v1:
time: 319 us
  Pallas kernels  311 us (97%)
  local copies, waits for them, and re-layouts  7.17 us (2%)
    pallas_call x1, Pallas kernels, decoder(): pl.pallas_call(functools.partial(decoder_kernel, num_tx, num_ty, n_layers...  311 us

profile of v1, /device:TPU:97, one launch (start us, length us, event | category | flops | bytes accessed | tf_op | source)
XLA Modules:
  0.0 318.6 jit_solution(2105918805927114273)
XLA Ops:
  0.6 1.3 reshape.12.pos_ref
  2.0 310.8 %decoder.1 = (bf16[64,4096]{1,0:T(8,128)(2,1)}, bf16[2,1024,2,128]{3,2,1,0:T(2,128)(2,1)}, bf16[2,1024,2,128]{3,2,1,0:T(2,128)(2,1)}) custom-call(bf16[64,4096]{1,0:T(8,128)(2,1)} %bitcast.3, bf16[2,64]{1,0:T(2,128)(2,1)} %g1_ref.1, bf16[2,64]{1,0:T(2,128)(2,1)} %b1_ref.1, bf16[2,64]{1,0:T(2,128)(2,1)} %g2_ref.1, bf16[2,64]{1,0:T(2,128)(2,1)} %b2_ref.1, ...), custom_call_target="tpu_custom_call" | custom-call | tf_op jit(solution)/shard_map/decoder/pallas_call | solution.py:710
  312.7 0.0 copy-start
  312.7 2.0 copy.24
  314.7 2.9 copy.25
  317.6 0.0 copy-done
  317.6 1.0 copy.26
Async XLA Ops:
  312.7 4.9 %copy-start = (bf16[2,1024,2,128]{3,2,1,0:T(2,128)(2,1)S(1)}, bf16[2,1024,2,128]{3,2,1,0:T(2,128)(2,1)}, u32[]{:S(2)}) copy-start(bf16[2,1024,2,128]{3,2,1,0:T(2,128)(2,1)} %get-tuple-element.14) | copy-start | bytes 3145732

commit v2 on v1

--- a/solution.py
+++ b/solution.py
@@ -14,6 +14,7 @@
 LOG2E = 1.4426950408889634
 LANES = 128
 BK = 1024
+SEND, RECV = 0, 1
 
 
 def rows_norm(x_f32, gain, bias):
@@ -96,17 +97,25 @@
     def out(self, i):
         chip, half, to, _ = self.plan[i]
         ref = self.view(chip, self.p.c, half)
-        return remote(ref, ref, self.sems.at[0, i], self.sems.at[1, i], to)
+        return remote(ref, ref, self.sems.at[SEND, i], self.sems.at[RECV, i], to)
 
     def arrived(self, i):
         _, half, to, chip = self.plan[i]
         core = self.p.c if i < 6 else 1 - self.p.c
         ref = self.view(chip, core, half)
-        remote(ref, ref, self.sems.at[0, i], self.sems.at[1, i], to).wait_recv()
+        remote(ref, ref, self.sems.at[SEND, i], self.sems.at[RECV, i], to).wait_recv()
+
+    def start_first(self):
+        for i in (6, 7, 0, 1):
+            self.out(i).start()
+
+    def start_second(self):
+        for i in (2, 3):
+            self.out(i).start()
 
     def start(self):
-        for i in (6, 7, 0, 1, 2, 3):
-            self.out(i).start()
+        self.start_first()
+        self.start_second()
 
     def own(self):
         self.arrived(6)
@@ -165,19 +174,19 @@
         half, to = ((0, p.above), (1, p.below), (1, p.above), (0, p.below), (0, p.above), (1, p.below))[i]
         here = src(half) if i < 4 else dst(down if i == 4 else up, half)
         there = dst((p.y, p.y, p.y, p.y, down, up)[i], half)
-        return remote(here, there, self.sems.at[0, n * self.SEMS + i], self.sems.at[1, n * self.SEMS + i], to)
+        return remote(here, there, self.sems.at[SEND, n * self.SEMS + i], self.sems.at[RECV, n * self.SEMS + i], to)
 
     def arrived(self, n, i):
         p = self.p
         src, dst = self.pieces[n]
         up, down, far = p.side(1), p.side(p.num_tx - 1), p.side(2)
         half, frm = ((0, down), (1, up), (1, down), (0, up), (0, far), (1, far))[i]
-        remote(src(half), dst(frm, half), self.sems.at[0, n * self.SEMS + i], self.sems.at[1, n * self.SEMS + i],
+        remote(src(half), dst(frm, half), self.sems.at[SEND, n * self.SEMS + i], self.sems.at[RECV, n * self.SEMS + i],
                p.above).wait_recv()
 
     def own(self, n, half):
         src, dst = self.pieces[n]
-        return pltpu.make_async_copy(src(half), dst(self.p.y, half), self.sems.at[1, n * self.SEMS + 6 + half])
+        return pltpu.make_async_copy(src(half), dst(self.p.y, half), self.sems.at[RECV, n * self.SEMS + 6 + half])
 
     def start_first(self):
         for i in (0, 1):
@@ -200,27 +209,29 @@
         self.start_first()
         self.start_second()
 
-    def relay(self):
-        for n in range(len(self.pieces)):
+    def relay(self, which=None):
+        for n in range(len(self.pieces)) if which is None else which:
             self.arrived(n, 0)
             self.copy(n, 4).start()
             self.arrived(n, 1)
             self.copy(n, 5).start()
 
-    def shard(self, k):
-        for n in range(len(self.pieces)):
-            if k == 0:
+    def step(self, j, which=None):
+        for n in range(len(self.pieces)) if which is None else which:
+            if j == 0:
                 self.own(n, 0).wait()
                 self.own(n, 1).wait()
-            elif k == 2:
-                self.arrived(n, 4)
-                self.arrived(n, 5)
-            else:
-                self.arrived(n, 3 if k == 1 else 2)
+            elif j > 1:
+                self.arrived(n, 2 * j - 2)
+                self.arrived(n, 2 * j - 1)
+
+    def piece(self, n):
+        for j in range(4):
+            self.step(j, [n])
 
     def finish(self):
-        for k in (0, 1, 3, 2):
-            self.shard(k)
+        for j in range(4):
+            self.step(j)
 
     def drain(self):
         for n in range(len(self.pieces)):
@@ -232,13 +243,13 @@
 
 
 def decoder_kernel(num_tx, num_ty, n_layers,
-                   xt_hbm, g1_ref, b1_ref, g2_ref, b2_ref, bo_ref, bd_ref, bup_ref, bq_ref, bk_ref, bv_ref, pos_ref,
+                   xt_hbm, g1_ref, b1_ref, g2_ref, b2_ref, bo_ref, bd_ref, bup_ref, bq_ref, bk_ref, bv_ref, pos_hbm,
                    wq_hbm, wk_hbm, wv_hbm, wo_hbm, wu_hbm, wd_hbm,
-                   yt_ref, kc_ref, vc_ref,
-                   xt, vrow, vloc, vbuf, vec, bloc, bup, raw, ws, w, wu, wd, wo, cs, a_all, hid, st, sv, kt, vt, qh, ob, obuf,
+                   yt_hbm, kc_hbm, vc_hbm, go_hbm,
+                   pos, xt, vrow, vloc, vbuf, vec, bloc, bup, raw, ws, w, wu, wd, wo, cs, a_all, hid, st, sv, kc, vc, kt, vt, qh, ob, obuf,
                    g, full, sibin, far_in, fin,
                    x_sems, v_sems, b_sems, y_sems, a_sems, u_sems, wq_sems, wo_sems, wx_sems, wu_sems, wd_sems,
-                   kv_sems, o_sems, p_sems, r_sems, l_sems):
+                   kv_sems, o_sems, p_sems, r_sems, l_sems, c_sems):
     p = Place(num_tx, num_ty)
     n_dev = num_tx * num_ty
     n_chip, x, y, c, ty = p.n_chip, p.x, p.y, p.c, p.ty
@@ -267,13 +278,14 @@
             ws[l, i] = raw[i].reshape(ws.shape[2], loc_w)
     for ld in load_raw(0):
         ld.start()
+    load_pos = pltpu.make_async_copy(pos_hbm, pos, l_sems.at[3])
+    load_pos.start()
     vrow[...] = jnp.zeros_like(vrow)
     for i, ref in enumerate((g1_ref, b1_ref, g2_ref, b2_ref, bo_ref, bd_ref)):
         vrow[i * n_layers:(i + 1) * n_layers, :piece_w] = ref[...].astype(F32)
     vloc[...] = vrow[...].astype(BF16)
     bloc[...] = jnp.zeros_like(bloc)
     bloc[:n_layers, :] = bup_ref[...].astype(F32)
-    flatten(0)
     pl.semaphore_wait(barrier, n_dev - 1)
 
     def halves(ref, l, n):
@@ -284,7 +296,6 @@
 
     qkv_rows = ws.shape[2]
     up_rows = wu_hbm.shape[1]
-    down_rows = wd_hbm.shape[1]
     o_rows = wo_hbm.shape[1]
 
     def gather_qkv(l):
@@ -298,16 +309,22 @@
                                 for at_c in (pl.ds(0, half), pl.ds(half, half))], wu_sems, early=1)
 
     def gather_down(l):
-        n = down_rows // 2
-        return ColumnGather(p, [(halves(wd_hbm, l, n), lambda ys, h: wd.at[ys, pl.ds(h * n, n)])], wd_sems)
+        n = col_w // 2
+        return ColumnGather(p, [((lambda h: wd_hbm.at[l, :, pl.ds(h * n, n)]), lambda ys, h: wd.at[ys, :, pl.ds(h * n, n)])],
+                            wd_sems)
+
+    def whole_o(l):
+        return wo if l == 0 else go_hbm.at[l - 1]
 
     def gather_o(l):
         n = o_rows // 2
-        return ColumnGather(p, [(halves(wo_hbm, l, n), lambda ys, h: wo.at[ys, rows(ty * o_rows + h * n, n)])], wo_sems)
+        return ColumnGather(p, [(halves(wo_hbm, l, n), lambda ys, h: whole_o(l).at[ys, rows(ty * o_rows + h * n, n)])],
+                            wo_sems.at[l])
 
     def spread_o(l):
         n = num_tx // 2
-        return RingGather(p, lambda chip, core, h: wo.at[pl.ds(h * n, n), rows((chip * 2 + core) * o_rows, o_rows)], wx_sems)
+        return RingGather(p, lambda chip, core, h: whole_o(l).at[pl.ds(h * n, n), rows((chip * 2 + core) * o_rows, o_rows)],
+                          wx_sems.at[l])
 
     g_qkv = [gather_qkv(l) for l in range(n_layers)]
     g_up = [gather_up(l) for l in range(n_layers)]
@@ -316,38 +333,42 @@
     s_o = [spread_o(l) for l in range(n_layers)]
 
     for d, to in zip(ids, devs):
-        remote(xt_hbm.at[:, rows(d * n_row, n_row)], xt.at[rows(p.me * piece_w, piece_w)], x_sems.at[0], x_sems.at[1], to).start()
-        remote(vloc, vbuf.at[p.me], v_sems.at[0], v_sems.at[1], to).start()
+        remote(xt_hbm.at[:, rows(d * n_row, n_row)], xt.at[rows(p.me * piece_w, piece_w)], x_sems.at[SEND], x_sems.at[RECV], to).start()
+        remote(vloc, vbuf.at[p.me], v_sems.at[SEND], v_sems.at[RECV], to).start()
     g_o[0].start()
+    flatten(0)
     g_qkv[0].start_first()
-    pltpu.make_async_copy(xt_hbm.at[:, rows(p.me * n_row, n_row)], xt.at[rows(p.me * piece_w, piece_w)], x_sems.at[1]).start()
-    pltpu.make_async_copy(vloc, vbuf.at[p.me], v_sems.at[1]).start()
+    pltpu.make_async_copy(xt_hbm.at[:, rows(p.me * n_row, n_row)], xt.at[rows(p.me * piece_w, piece_w)], x_sems.at[RECV]).start()
+    pltpu.make_async_copy(vloc, vbuf.at[p.me], v_sems.at[RECV]).start()
     bup_w = bup_ref.shape[1]
     for k in range(1, num_tx):
-        remote(bloc, bup.at[:, rows(y * bup_w, bup_w)], b_sems.at[0], b_sems.at[1], p.over(k)).start()
-    pltpu.make_async_copy(bloc, bup.at[:, rows(y * bup_w, bup_w)], b_sems.at[1]).start()
+        remote(bloc, bup.at[:, rows(y * bup_w, bup_w)], b_sems.at[SEND], b_sems.at[RECV], p.over(k)).start()
+    pltpu.make_async_copy(bloc, bup.at[:, rows(y * bup_w, bup_w)], b_sems.at[RECV]).start()
     for l in range(1, n_layers):
         for ld in load_raw(l):
             ld.start()
         flatten(l)
 
+    load_pos.wait()
     lane = lax.broadcasted_iota(jnp.int32, (1, head_w), 1)
     inv_freq = jnp.exp(lax.rem(lane, head_w // 2).astype(F32) * (-2.0 * math.log(ROPE_THETA) / head_w))
     sign = jnp.where(lane < head_w // 2, -1.0, 1.0)
 
+    def positions(b):
+        return pos[rows(b * blk, blk)].reshape(1, blk)
+
     def angles(k, carry):
-        pos = pos_ref[pl.ds(y * n_chip + k, 1), :].astype(F32)
-        ang = jnp.broadcast_to(pos, (head_w, blk)).T * inv_freq
+        ang = jnp.broadcast_to(positions(y * n_chip + k).astype(F32), (head_w, blk)).T * inv_freq
         cs[0, rows(k * blk, blk), :] = jnp.cos(ang)
         cs[1, rows(k * blk, blk), :] = jnp.sin(ang) * sign
         return carry
     lax.fori_loop(0, n_chip, angles, 0)
-    took(vbuf, v_sems.at[1])
+    took(vbuf, v_sems.at[RECV])
     per = LANES // piece_w
     for j in range(width // LANES):
         vec[:, j * LANES:(j + 1) * LANES] = jnp.concatenate(
             [vbuf[per * j + i][:, :piece_w].astype(F32) for i in range(per)], axis=1)
-    took(xt, x_sems.at[1])
+    took(xt, x_sems.at[RECV])
 
     def turn(j, carry):
         hid[:, rows(j * LANES, LANES)] = xt[rows(j * LANES, LANES), :].T
@@ -393,14 +414,14 @@
                 else:
                     sv[k, h] = v.T
             if i > 0:
-                (kc_ref, vc_ref)[i - 1][l, at_row] = jnp.concatenate(parts, axis=1).reshape(blk, loc_heads, head_w)
+                (kc, vc)[i - 1][l, at_row] = jnp.concatenate(parts, axis=1).reshape(blk, loc_heads, head_w)
         at_tok = rows((y * n_chip + slot) * blk, blk)
         par = lax.rem(slot, 2)
         at_q = rows((y * (n_chip // 2) + slot // 2) * blk, blk)
         for h in range(loc_heads):
             yd = c * loc_heads + h
             for r, (src, dst) in enumerate(((st.at[k, h, 1], kt.at[at_tok]), (sv.at[k, h], vt.at[:, at_tok]))):
-                copy_or_send(jnp.logical_and(yd == y, c == r), src, dst, kv_sems.at[0], kv_sems.at[1], p.at(yd, x * 2 + r))
+                copy_or_send(jnp.logical_and(yd == y, c == r), src, dst, kv_sems.at[SEND], kv_sems.at[RECV], p.at(yd, x * 2 + r))
             copy_or_send(jnp.logical_and(yd == y, c == par), st.at[k, h, 0], qh.at[at_q], kv_sems.at[2], kv_sems.at[3],
                          p.at(yd, x * 2 + par))
 
@@ -416,7 +437,7 @@
             q_col = lax.broadcasted_iota(jnp.int32, (1, blk), 1)
             at_q = [(2 * (2 * grp + i) + c) for i in range(2)]
             q_pos = jnp.concatenate([q_col + b * blk for b in at_q], axis=1)
-            first = q_pos - jnp.concatenate([pos_ref[pl.ds(b, 1), :] for b in at_q], axis=1)
+            first = q_pos - jnp.concatenate([positions(b) for b in at_q], axis=1)
             key = lax.broadcasted_iota(jnp.int32, (blk, q_grp), 0)
             scale = head_w ** -0.5 * LOG2E
 
@@ -453,8 +474,8 @@
                 yt, xd = b // n_chip, lax.rem(b, n_chip)
                 for r in range(2):
                     here = jnp.logical_and(jnp.logical_and(yt == y, xd == x), c == r)
-                    copy_or_send(here, ob.at[2 * grp + i, pl.ds(r * n_row, n_row)], obuf.at[:, cols_o], o_sems.at[0],
-                                 o_sems.at[1], p.at(yt, xd * 2 + r))
+                    copy_or_send(here, ob.at[2 * grp + i, pl.ds(r * n_row, n_row)], obuf.at[:, cols_o], o_sems.at[SEND],
+                                 o_sems.at[RECV], p.at(yt, xd * 2 + r))
             for at_n, hook in hooks.items():
                 @pl.when(n == at_n)
                 def _():
@@ -463,82 +484,94 @@
             return carry
         lax.fori_loop(0, n_grp, step, 0)
 
-    def up(l, k):
-        slot = p.chip(k)
-
-        def part(n, carry):
-            cc = rows(n * 512, 512)
-            h = jnp.dot(a_all[slot], wu[:, cc], preferred_element_type=F32) + bup[l:l + 1, cc]
-            g[k, :, cc] = gelu_tanh(h).astype(BF16)
-            return carry
-        lax.fori_loop(0, wu.shape[1] // 512, part, 0)
-
-    blocks = (0, 1, last, 2)
-    cols = [rows(p.side(k) * col_w, col_w) for k in blocks]
+    def up(l, k, n):
+        half = wu.shape[1] // 2
+        cc = pl.ds(n * half, half)
+        h = jnp.dot(a_all[p.chip(k)], wu[:, cc], preferred_element_type=F32) + bup[l:l + 1, cc]
+        g[k, :, cc] = gelu_tanh(h).astype(BF16)
+
+    half_col = col_w // 2
+    below, above, far_side = p.side(num_tx - 1), p.side(1), p.side(2)
+    blocks = (((y, 0), (y, 1)), ((below, 0), (above, 1)), ((below, 1), (above, 0)), ((far_side, 0), (far_side, 1)))
+    cols = [[rows(t * col_w + h * half_col, half_col) for t, h in pair] for pair in blocks]
     top, bottom = rows(c * n_row, half_row), rows(c * n_row + half_row, half_row)
 
     def to_sibling(k, j):
-        i = k * num_tx + j
-        return remote(full.at[k, other, cols[j]], sibin.at[k, :, cols[j]], p_sems.at[0, i], p_sems.at[1, i], p.sib)
+        out = []
+        for i in range(2):
+            at_s = (k * num_tx + j) * 2 + i
+            out.append(remote(full.at[k, other, cols[j][i]], sibin.at[k, :, cols[j][i]], p_sems.at[SEND, at_s], p_sems.at[RECV, at_s],
+                              p.sib))
+        return out
 
     def rs(kind, j):
         k, part, dst, to = ((1, bottom, fin.at[0], p.right), (last, top, fin.at[1], p.left), (2, top, far_in.at[0], p.right),
                             (2, bottom, far_in.at[1], p.left), (1, top, fin.at[2], p.right),
                             (last, bottom, fin.at[3], p.left))[kind]
-        i = kind * num_tx + j
-        return remote(full.at[k, part, cols[j]], dst.at[:, cols[j]], r_sems.at[0, i], r_sems.at[1, i], to)
-
-    def partials(j):
-        def part(n, carry):
-            k = order(lax.rem(n + 1, n_chip))
-            full[k, :, cols[j]] = jnp.dot(g[k], wd[p.side(blocks[j])], preferred_element_type=F32)
-            to_sibling(k, j).start()
-            return carry
-        lax.fori_loop(0, n_chip, part, 0)
+        out = []
+        for i in range(2):
+            at_s = (kind * num_tx + j) * 2 + i
+            out.append(remote(full.at[k, part, cols[j][i]], dst.at[:, cols[j][i]], r_sems.at[SEND, at_s], r_sems.at[RECV, at_s], to))
+        return out
+
+    def start(copies):
+        for cp in copies:
+            cp.start()
+
+    def landed(copies):
+        for cp in copies:
+            cp.wait_recv()
+
+    def partial(k, j):
+        for i, (t, h) in enumerate(blocks[j]):
+            full[k, :, cols[j][i]] = jnp.dot(g[k], wd[t, :, h * half_col:(h + 1) * half_col], preferred_element_type=F32)
+        start(to_sibling(k, j))
 
     def pair_sum(k, j):
-        to_sibling(k, j).wait_recv()
-        full[k, mine, cols[j]] = full[k, mine, cols[j]] + sibin[k, :, cols[j]]
-
-    def send_partials(j):
+        landed(to_sibling(k, j))
+        for cc in cols[j]:
+            full[k, mine, cc] = full[k, mine, cc] + sibin[k, :, cc]
+
+    def send_near(j):
         pair_sum(1, j)
-        rs(S_DIRECT_R, j).start()
+        start(rs(S_DIRECT_R, j))
         pair_sum(last, j)
-        rs(S_DIRECT_L, j).start()
+        start(rs(S_DIRECT_L, j))
+
+    def send_far(j):
         pair_sum(2, j)
-        rs(S_FAR_R, j).start()
-        rs(S_FAR_L, j).start()
+        start(rs(S_FAR_R, j))
+        start(rs(S_FAR_L, j))
         pair_sum(0, j)
 
     def pass_on(j):
-        rs(S_FAR_R, j).wait_recv()
-        full[1, top, cols[j]] = full[1, top, cols[j]] + far_in[0, :, cols[j]]
-        rs(S_SUM_R, j).start()
-        rs(S_FAR_L, j).wait_recv()
-        full[last, bottom, cols[j]] = full[last, bottom, cols[j]] + far_in[1, :, cols[j]]
-        rs(S_SUM_L, j).start()
+        landed(rs(S_FAR_R, j))
+        for cc in cols[j]:
+            full[1, top, cc] = full[1, top, cc] + far_in[0, :, cc]
+        start(rs(S_SUM_R, j))
+        landed(rs(S_FAR_L, j))
+        for cc in cols[j]:
+            full[last, bottom, cc] = full[last, bottom, cc] + far_in[1, :, cc]
+        start(rs(S_SUM_L, j))
 
     def complete(l, j):
-        cc = cols[j]
-        bias = vec[5 * n_layers + l:5 * n_layers + l + 1, cc]
         for kind in (S_DIRECT_R, S_DIRECT_L, S_SUM_R, S_SUM_L):
-            rs(kind, j).wait_recv()
-        for part, out, ins in ((top, pl.ds(0, half_row), (1, 2)), (bottom, pl.ds(half_row, half_row), (0, 3))):
-            tot = full[0, part, cc] + fin[ins[0], :, cc] + fin[ins[1], :, cc]
-            hid[out, cc] = (hid[out, cc].astype(F32) + tot + bias).astype(BF16)
+            landed(rs(kind, j))
+        for cc in cols[j]:
+            bias = vec[5 * n_layers + l:5 * n_layers + l + 1, cc]
+            for part, out, ins in ((top, pl.ds(0, half_row), (1, 2)), (bottom, pl.ds(half_row, half_row), (0, 3))):
+                tot = full[0, part, cc] + fin[ins[0], :, cc] + fin[ins[1], :, cc]
+                hid[out, cc] = (hid[out, cc].astype(F32) + tot + bias).astype(BF16)
 
     def give_back(j):
-        row = p.side(blocks[j])
-
-        def turn_back(n, carry):
-            at_c = rows(row * col_w + n * LANES, LANES)
-            xt[at_c, :] = hid[:, at_c].T
-            return carry
-        lax.fori_loop(0, col_w // LANES, turn_back, 0)
-        for k in range(num_ty):
-            to_ty = lax.rem(ty + k, num_ty)
-            copy_or_send(jnp.logical_and(row == y, k == 0), xt.at[rows((row * num_ty + to_ty) * piece_w, piece_w)],
-                         yt_ref.at[:, rows(p.me * n_row, n_row)], y_sems.at[0], y_sems.at[1], p.at(row, to_ty))
+        for t, h in blocks[j]:
+            for n in range(half_col // LANES):
+                at_c = rows(t * col_w + h * half_col + n * LANES, LANES)
+                xt[at_c, :] = hid[:, at_c].T
+            for k in range(num_ty // 2):
+                to_ty = h * (num_ty // 2) + k
+                copy_or_send(jnp.logical_and(t == y, ty == to_ty), xt.at[rows((t * num_ty + to_ty) * piece_w, piece_w)],
+                             yt_hbm.at[:, rows(p.me * n_row, n_row)], y_sems.at[SEND], y_sems.at[RECV], p.at(t, to_ty))
 
     def start_forward():
         @pl.when(c == 0)
@@ -554,11 +587,14 @@
         a_all[x, mine, :] = rows_norm(hid[...].astype(F32), vector(0, l), vector(1, l))
         ga = row_gather(a_sems)
         ga.start()
+        ahead = [] if last_layer else [g_o[l + 1].relay]
         if first_layer:
             g_o[l].relay()
             g_qkv[l].start_second()
             ga.relay()
             g_qkv[l].relay()
+            if not last_layer:
+                g_o[l + 1].start()
             ga.own()
             ga.near()
             g_o[l].finish()
@@ -569,29 +605,37 @@
             ga.far_done()
             ga.drain()
             g_qkv[l].finish()
-            each(0, n_chip, lambda k: project(l, k), {})
+            each(0, n_chip, lambda k: project(l, k), {2: ahead})
+            s_o[l].relay()
         else:
-            g_qkv[l].relay()
+            if not last_layer:
+                g_o[l + 1].start()
             ga.relay()
             ga.own()
-            g_o[l].finish()
-            s_o[l].start()
+            s_o[l].start_second()
+            s_o[l].relay()
             g_qkv[l].finish()
-            each(0, last, lambda k: project(l, k), {1: [ga.near, ga.near_right, ga.near_left]})
+            each(0, last, lambda k: project(l, k), {1: [ga.near, ga.near_right, ga.near_left], 2: ahead})
             ga.far()
             ga.far_done()
             ga.drain()
             project(l, 2)
+        for i, (src, dst) in enumerate(((kc, kc_hbm), (vc, vc_hbm))):
+            pltpu.make_async_copy(src.at[l], dst.at[l], c_sems.at[i]).start()
+        if not last_layer:
+            g_o[l + 1].finish()
+            s_o[l + 1].start_first()
+        sent_away(p, kt, qh, kv_sems, loc_heads)
         g_up[l].start_first()
-        s_o[l].relay()
-        took(kt, kv_sems.at[1])
+        took(kt, kv_sems.at[RECV])
         start_forward()
         took(qh, kv_sems.at[3])
         took(kt, kv_sems.at[5])
         took(kt, kv_sems.at[4])
         attend({0: [s_o[l].near]})
+        g_up[l].relay([0])
         g_up[l].start_second()
-        g_up[l].relay()
+        g_up[l].relay([1])
         g_qkv[l].drain()
         g_down[l].start()
         s_o[l].far()
@@ -599,7 +643,12 @@
         s_o[l].near_right()
         s_o[l].near_left()
         s_o[l].far_done()
-        took(obuf, o_sems.at[1])
+        load_o = [] if first_layer else [pltpu.make_async_copy(whole_o(l).at[t], wo.at[t], l_sems.at[t]) for t in range(num_tx)]
+        for ld in load_o:
+            ld.start()
+        took(obuf, o_sems.at[RECV])
+        for ld in load_o:
+            ld.wait()
 
         def out_product(t, carry):
             cc = rows(t * col_w, col_w)
@@ -611,52 +660,78 @@
         gu = row_gather(u_sems)
         gu.start()
         if first_layer:
-            took(bup, b_sems.at[1])
+            took(bup, b_sems.at[RECV])
         gu.own()
         gu.relay()
-        g_up[l].finish()
-        each(0, n_chip, lambda k: up(l, k), {1: [gu.near, gu.near_right, gu.near_left], last: [gu.far, gu.far_done]})
+        g_up[l].piece(0)
+        each(0, last, lambda k: up(l, k, 0), {1: [gu.near, gu.near_right, gu.near_left]})
+        if not first_layer:
+            gu.far()
+            gu.far_done()
+            up(l, 2, 0)
+        g_up[l].piece(1)
+        g_down[l].step(0)
+
+        def near_partial(n, carry):
+            up(l, order(n), 1)
+            partial(order(n), 0)
+            return carry
+        lax.fori_loop(1, last, near_partial, 0)
+        if first_layer:
+            gu.far()
+            gu.far_done()
+            up(l, 2, 0)
+        up(l, 2, 1)
         gu.drain()
         s_o[l].drain()
         g_o[l].drain()
         g_up[l].drain()
+        send_near(0)
+        partial(2, 0)
+        up(l, 0, 1)
+        partial(0, 0)
         g_down[l].relay()
         if not last_layer:
-            g_qkv[l + 1].start_first()
-        for j in range(num_tx):
-            g_down[l].shard(blocks[j])
-            if j == num_tx - 1 and not last_layer:
-                g_o[l + 1].start()
-            partials(j)
-            send_partials(j)
-            if j > 0:
-                pass_on(j - 1)
+            g_qkv[l + 1].start()
+        send_far(0)
+        for j in range(1, num_tx):
+            g_down[l].step(j)
+
+            def each_partial(n, carry):
+                partial(order(lax.rem(n + 1, n_chip)), j)
+                return carry
+            lax.fori_loop(0, n_chip, each_partial, 0)
+            send_near(j)
+            send_far(j)
+            pass_on(j - 1)
             if j > 1:
                 complete(l, j - 2)
                 if last_layer:
                     give_back(j - 2)
+        pass_on(num_tx - 1)
         if not last_layer:
-            g_o[l + 1].relay()
-            g_qkv[l + 1].start_second()
-        pass_on(num_tx - 1)
+            g_qkv[l + 1].relay()
         for j in range(num_tx - 2, num_tx):
             complete(l, j)
             if last_layer:
                 give_back(j)
         for j in range(num_tx):
             for k in range(n_chip):
-                to_sibling(k, j).wait_send()
+                for cp in to_sibling(k, j):
+                    cp.wait_send()
             for kind in range(6):
-                rs(kind, j).wait_send()
+                for cp in rs(kind, j):
+                    cp.wait_send()
         g_down[l].drain()
-        sent_away(p, kt, qh, kv_sems, loc_heads)
         o_away(p, obuf, o_sems, head_w)
 
-    took(xt_hbm.at[:, pl.ds(0, (n_dev - 1) * n_row)], x_sems.at[0])
-    took(vbuf.at[pl.ds(0, n_dev - 1)], v_sems.at[0])
-    took(bup.at[:, pl.ds(0, (num_tx - 1) * bup_w)], b_sems.at[0])
-    took(yt_ref, y_sems.at[1])
-    took(xt.at[pl.ds(0, (n_dev - 1) * piece_w)], y_sems.at[0])
+    took(kc_hbm, c_sems.at[SEND])
+    took(vc_hbm, c_sems.at[RECV])
+    took(xt_hbm.at[:, pl.ds(0, (n_dev - 1) * n_row)], x_sems.at[SEND])
+    took(vbuf.at[pl.ds(0, n_dev - 1)], v_sems.at[SEND])
+    took(bup.at[:, pl.ds(0, (num_tx - 1) * bup_w)], b_sems.at[SEND])
+    took(yt_hbm, y_sems.at[RECV])
+    took(xt.at[pl.ds(0, (n_dev - 1) * piece_w)], y_sems.at[SEND])
 
 
 def sent_away(p, kt, qh, kv_sems, loc_heads):
@@ -666,12 +741,12 @@
 
     @pl.when(stays)
     def _():
-        took(kt.at[pl.ds(0, n_tok * 3 // 4)], kv_sems.at[0])
+        took(kt.at[pl.ds(0, n_tok * 3 // 4)], kv_sems.at[SEND])
         took(qh.at[pl.ds(0, n_q * 3 // 4)], kv_sems.at[2])
 
     @pl.when(jnp.logical_not(stays))
     def _():
-        took(kt, kv_sems.at[0])
+        took(kt, kv_sems.at[SEND])
         took(qh, kv_sems.at[2])
 
 
@@ -680,11 +755,11 @@
 
     @pl.when(stays)
     def _():
-        took(obuf.at[:, pl.ds(0, obuf.shape[1] - head_w)], o_sems.at[0])
+        took(obuf.at[:, pl.ds(0, obuf.shape[1] - head_w)], o_sems.at[SEND])
 
     @pl.when(jnp.logical_not(stays))
     def _():
-        took(obuf, o_sems.at[0])
+        took(obuf, o_sems.at[SEND])
 
 
 def decoder(num_tx, num_ty, xt, vectors, b_up, b_qkv, pos, wq, wk, wv, wo, wu, wd):
@@ -705,30 +780,64 @@
     hb = pl.BlockSpec(memory_space=pl.ANY)
     V = pltpu.VMEM
     dma = pltpu.SemaphoreType.DMA
+    ends = dma((2,))
     cache = jax.ShapeDtypeStruct((n_layers, tok_loc, loc_heads, head_w), BF16)
     CG, RG = ColumnGather.SEMS, RingGather.SEMS
     return pl.pallas_call(
         functools.partial(decoder_kernel, num_tx, num_ty, n_layers),
-        out_shape=(jax.ShapeDtypeStruct((piece_w, n_tok), BF16), cache, cache),
-        in_specs=[hb] + [vm] * 11 + [hb] * 6,
-        out_specs=(vm,) * 3,
-        scratch_shapes=[V((width, n_row), BF16), V((n_vec, LANES), F32), V((n_vec, LANES), BF16), V((n_dev, n_vec, LANES), BF16),
+        out_shape=(jax.ShapeDtypeStruct((piece_w, n_tok), BF16), cache, cache,
+                   jax.ShapeDtypeStruct((max(n_layers - 1, 1), num_tx, width, col_w), BF16)),
+        in_specs=[hb] + [vm] * 10 + [hb] * 7,
+        out_specs=(hb,) * 4,
+        scratch_shapes=[V((n_tok,), jnp.int32), V((width, n_row), BF16), V((n_vec, LANES), F32), V((n_vec, LANES), BF16), V((n_dev, n_vec, LANES), BF16),
                         V((n_vec, width), F32), V((8, b_up.shape[1]), F32), V((8, ff), F32),
                         V((3, d_rows, loc_heads, head_w), BF16), V((n_layers, 3, d_rows, loc_w), BF16),
                         V((width, 3 * loc_w), BF16), V((width, ff), BF16), V((num_tx, ff, col_w), BF16),
                         V((num_tx, width, col_w), BF16), V((2, tok_loc, head_w), F32),
                         V((n_chip, blk, width), BF16), V((n_row, width), BF16),
-                        V((n_chip, loc_heads, 2, blk, head_w), BF16), V((n_chip, loc_heads, head_w, blk), BF16),
+                        V((n_chip, loc_heads, 2, blk, head_w), BF16), V((n_chip, loc_heads, head_w, blk), BF16), V(cache.shape, BF16),
+                        V(cache.shape, BF16),
                         V((n_tok, head_w), BF16), V((head_w, n_tok), BF16), V((n_q * blk, head_w), BF16),
                         V((n_q, blk, head_w), BF16), V((n_row, width), BF16), V((n_chip, blk, ff), BF16),
                         V((n_chip, blk, width), F32), V((n_chip, n_row, width), F32),
                         V((2, n_row // 2, width), F32), V((4, n_row // 2, width), F32),
-                        dma((2,)), dma((2,)), dma((2,)), dma((2,)), dma((2, RG)), dma((2, RG)), dma((2, 3 * CG)), dma((2, CG)),
-                        dma((2, RG)), dma((2, 2 * CG)), dma((2, CG)), dma((6,)), dma((2,)), dma((2, n_chip * num_tx)),
-                        dma((2, 6 * num_tx)), dma((3,))],
+                        ends, ends, ends, ends, dma((2, RG)), dma((2, RG)), dma((2, 3 * CG)),
+                        dma((n_layers, 2, CG)), dma((n_layers, 2, RG)), dma((2, 2 * CG)), dma((2, CG)), dma((6,)), ends, dma((2, 2 * n_chip * num_tx)),
+                        dma((2, 12 * num_tx)), dma((4,)), ends],
         compiler_params=pltpu.CompilerParams(collective_id=1, has_side_effects=True, vmem_limit_bytes=63 << 20),
         name="decoder",
-    )(xt, *vectors, b_up, *b_qkv, pos, wq, wk, wv, wo, wu, wd)
+    )(xt, *vectors, b_up, *b_qkv, pos, wq, wk, wv, wo, wu, wd)[:3]
+
+
+def hand_over_kernel(n, *refs):
+    src, dst, buf, sems = refs[:n], refs[n:2 * n], refs[2 * n:3 * n], refs[3 * n]
+    copies = []
+    for i in range(n):
+        step = src[i].shape[0] // 2
+        for h in range(2):
+            part = pl.ds(h * step, step)
+            copies.append((pltpu.make_async_copy(src[i].at[part], buf[i].at[part], sems.at[SEND, 2 * i + h]),
+                           pltpu.make_async_copy(buf[i].at[part], dst[i].at[part], sems.at[RECV, 2 * i + h])))
+    for load, _ in copies:
+        load.start()
+    for load, store in copies:
+        load.wait()
+        store.start()
+    for _, store in copies:
+        store.wait()
+
+
+def hand_over(arrays):
+    n = len(arrays)
+    hb = pl.BlockSpec(memory_space=pl.ANY)
+    return pl.pallas_call(
+        functools.partial(hand_over_kernel, n),
+        out_shape=tuple(jax.ShapeDtypeStruct(a.shape, a.dtype) for a in arrays),
+        in_specs=[hb] * n,
+        out_specs=(hb,) * n,
+        scratch_shapes=[pltpu.VMEM(a.shape, a.dtype) for a in arrays] + [pltpu.SemaphoreType.DMA((2, 2 * n))],
+        name="hand_over",
+    )(*arrays)
 
 
 def solution(mesh):
@@ -746,11 +855,10 @@
 
     def device_fn(x_loc, seg_all, pos_all, ln1_gain, ln1_bias, w_q, b_q, w_k, b_k, w_v, b_v, w_o, b_o,
                   ln2_gain, ln2_bias, w_up, b_up, w_down, b_down):
-        n_tok = x_loc.shape[0]
-        blk = 2 * n_tok // (num_tx * num_ty)
         yt, k, v = decoder(num_tx, num_ty, x_loc.T, (ln1_gain, ln1_bias, ln2_gain, ln2_bias, b_o, b_down), b_up,
-                           (b_q, b_k, b_v), pos_all.reshape(-1, blk), w_q, w_k, w_v,
+                           (b_q, b_k, b_v), pos_all, w_q, w_k, w_v,
                            w_o.reshape(w_o.shape[0], -1, w_o.shape[-1]), w_up, w_down)
+        yt, k, v = hand_over((yt, k, v))
         return yt.T, k, v
 
     return jax.shard_map(device_fn, mesh=mesh, in_specs=in_specs, out_specs=out_specs, check_vma=False)

time: 319 us -> 304 us (0.953)
  Pallas kernels: 311 us -> 303 us
  local copies, waits for them, and re-layouts: 7.17 us -> 0 us
    pallas_call x1, Pallas kernels: 311 us -> 301 us  [decoder(): pl.pallas_call(functools.partial(decoder_kernel, num_tx, num_ty, n_layers...]
    unnamed x5 -> x0, local copies, waits for them, and re-layouts: 5.84 us -> none
where the time goes in v2:
time: 304 us
  Pallas kernels  303 us (100%)
    pallas_call x1, Pallas kernels, decoder(): pl.pallas_call(functools.partial(decoder_kernel, num_tx, num_ty, n_layers...  301 us

profile of v2, /device:TPU:97, one launch (start us, length us, event | category | flops | bytes accessed | tf_op | source)
XLA Modules:
  0.0 304.3 jit_solution(7408997590105020548)
XLA Ops:
  0.6 300.9 %decoder.1 = (bf16[64,4096]{1,0:T(8,128)(2,1)}, bf16[2,1024,2,128]{3,2,1,0:T(2,128)(2,1)}, bf16[2,1024,2,128]{3,2,1,0:T(2,128)(2,1)}, bf16[1,4,2048,512]{3,2,1,0:T(8,128)(2,1)}) custom-call(bf16[64,4096]{1,0:T(8,128)(2,1)} %bitcast.3, bf16[2,64]{1,0:T(2,128)(2,1)} %g1_ref.1, bf16[2,64]{1,0:T(2,128)(2,1)} %b1_ref.1, bf16[2,64]{1,0:T(2,128)(2,1)} %g2_ref.1, ...), custom_call_target="tpu_custom_call" | custom-call | tf_op jit(solution)/shard_map/decoder/pallas_call | solution.py:786
  301.5 2.6 hand_over.1

commit v3 on v2

--- a/solution.py
+++ b/solution.py
@@ -188,9 +188,13 @@
         src, dst = self.pieces[n]
         return pltpu.make_async_copy(src(half), dst(self.p.y, half), self.sems.at[RECV, n * self.SEMS + 6 + half])
 
-    def start_first(self):
+    def start_piece(self, n):
         for i in (0, 1):
-            for n in range(len(self.pieces)):
+            self.copy(n, i).start()
+
+    def start_first(self, n_from=0):
+        for i in (0, 1):
+            for n in range(n_from, len(self.pieces)):
                 self.copy(n, i).start()
         self.rest(range(self.early))
 
@@ -332,18 +336,23 @@
     g_o = [gather_o(l) for l in range(n_layers)]
     s_o = [spread_o(l) for l in range(n_layers)]
 
+    for k in range(1, num_tx):
+        remote(vloc, vbuf.at[y, ty], v_sems.at[SEND], v_sems.at[RECV], p.over(k)).start()
     for d, to in zip(ids, devs):
         remote(xt_hbm.at[:, rows(d * n_row, n_row)], xt.at[rows(p.me * piece_w, piece_w)], x_sems.at[SEND], x_sems.at[RECV], to).start()
-        remote(vloc, vbuf.at[p.me], v_sems.at[SEND], v_sems.at[RECV], to).start()
     g_o[0].start()
     flatten(0)
     g_qkv[0].start_first()
     pltpu.make_async_copy(xt_hbm.at[:, rows(p.me * n_row, n_row)], xt.at[rows(p.me * piece_w, piece_w)], x_sems.at[RECV]).start()
-    pltpu.make_async_copy(vloc, vbuf.at[p.me], v_sems.at[RECV]).start()
+    pltpu.make_async_copy(vloc, vbuf.at[y, ty], v_sems.at[RECV]).start()
     bup_w = bup_ref.shape[1]
     for k in range(1, num_tx):
         remote(bloc, bup.at[:, rows(y * bup_w, bup_w)], b_sems.at[SEND], b_sems.at[RECV], p.over(k)).start()
     pltpu.make_async_copy(bloc, bup.at[:, rows(y * bup_w, bup_w)], b_sems.at[RECV]).start()
+    column = vbuf.at[:, ty]
+    took(column, v_sems.at[RECV])
+    for k in range(1, num_ty):
+        remote(column, column, v_sems.at[2], v_sems.at[3], p.at(y, lax.rem(ty + k, num_ty))).start()
     for l in range(1, n_layers):
         for ld in load_raw(l):
             ld.start()
@@ -363,11 +372,11 @@
         cs[1, rows(k * blk, blk), :] = jnp.sin(ang) * sign
         return carry
     lax.fori_loop(0, n_chip, angles, 0)
-    took(vbuf, v_sems.at[RECV])
+    took(vbuf.at[:, pl.ds(1, num_ty - 1)], v_sems.at[3])
     per = LANES // piece_w
     for j in range(width // LANES):
         vec[:, j * LANES:(j + 1) * LANES] = jnp.concatenate(
-            [vbuf[per * j + i][:, :piece_w].astype(F32) for i in range(per)], axis=1)
+            [vbuf[(per * j + i) // num_ty, (per * j + i) % num_ty][:, :piece_w].astype(F32) for i in range(per)], axis=1)
     took(xt, x_sems.at[RECV])
 
     def turn(j, carry):
@@ -542,19 +551,18 @@
         pair_sum(2, j)
         start(rs(S_FAR_R, j))
         start(rs(S_FAR_L, j))
+
+    def pass_on(j):
+        for i, cc in enumerate(cols[j]):
+            rs(S_FAR_R, j)[i].wait_recv()
+            full[1, top, cc] = full[1, top, cc] + far_in[0, :, cc]
+            rs(S_SUM_R, j)[i].start()
+            rs(S_FAR_L, j)[i].wait_recv()
+            full[last, bottom, cc] = full[last, bottom, cc] + far_in[1, :, cc]
+            rs(S_SUM_L, j)[i].start()
+
+    def complete(l, j):
         pair_sum(0, j)
-
-    def pass_on(j):
-        landed(rs(S_FAR_R, j))
-        for cc in cols[j]:
-            full[1, top, cc] = full[1, top, cc] + far_in[0, :, cc]
-        start(rs(S_SUM_R, j))
-        landed(rs(S_FAR_L, j))
-        for cc in cols[j]:
-            full[last, bottom, cc] = full[last, bottom, cc] + far_in[1, :, cc]
-        start(rs(S_SUM_L, j))
-
-    def complete(l, j):
         for kind in (S_DIRECT_R, S_DIRECT_L, S_SUM_R, S_SUM_L):
             landed(rs(kind, j))
         for cc in cols[j]:
@@ -610,6 +618,7 @@
         else:
             if not last_layer:
                 g_o[l + 1].start()
+            g_up[l].start_piece(0)
             ga.relay()
             ga.own()
             s_o[l].start_second()
@@ -626,28 +635,34 @@
             g_o[l + 1].finish()
             s_o[l + 1].start_first()
         sent_away(p, kt, qh, kv_sems, loc_heads)
-        g_up[l].start_first()
+        g_up[l].start_first(0 if first_layer else 1)
         took(kt, kv_sems.at[RECV])
         start_forward()
         took(qh, kv_sems.at[3])
         took(kt, kv_sems.at[5])
         took(kt, kv_sems.at[4])
-        attend({0: [s_o[l].near]})
+        by_chip = [] if first_layer else [
+            pltpu.make_async_copy(whole_o(l).at[:, at_r], wo.at[:, at_r], l_sems.at[i])
+            for i, at_r in enumerate(rows(p.chip(k) * 2 * o_rows, 2 * o_rows) for k in range(n_chip))]
+
+        def near_o():
+            s_o[l].own()
+            s_o[l].near_right()
+            s_o[l].near_left()
+            for k in (0, 1, last):
+                for ld in by_chip[k:k + 1]:
+                    ld.start()
+        attend({0: [s_o[l].near], 1: [near_o, s_o[l].far]})
         g_up[l].relay([0])
         g_up[l].start_second()
         g_up[l].relay([1])
         g_qkv[l].drain()
         g_down[l].start()
-        s_o[l].far()
-        s_o[l].own()
-        s_o[l].near_right()
-        s_o[l].near_left()
         s_o[l].far_done()
-        load_o = [] if first_layer else [pltpu.make_async_copy(whole_o(l).at[t], wo.at[t], l_sems.at[t]) for t in range(num_tx)]
-        for ld in load_o:
+        for ld in by_chip[2:3]:
             ld.start()
         took(obuf, o_sems.at[RECV])
-        for ld in load_o:
+        for ld in by_chip:
             ld.wait()
 
         def out_product(t, carry):
@@ -698,11 +713,11 @@
             g_down[l].step(j)
 
             def each_partial(n, carry):
-                partial(order(lax.rem(n + 1, n_chip)), j)
+                partial(lax.rem(2 + last * n, n_chip), j)
                 return carry
             lax.fori_loop(0, n_chip, each_partial, 0)
+            send_far(j)
             send_near(j)
-            send_far(j)
             pass_on(j - 1)
             if j > 1:
                 complete(l, j - 2)
@@ -728,7 +743,8 @@
     took(kc_hbm, c_sems.at[SEND])
     took(vc_hbm, c_sems.at[RECV])
     took(xt_hbm.at[:, pl.ds(0, (n_dev - 1) * n_row)], x_sems.at[SEND])
-    took(vbuf.at[pl.ds(0, n_dev - 1)], v_sems.at[SEND])
+    took(vbuf.at[pl.ds(0, num_tx - 1), 0], v_sems.at[SEND])
+    took(vbuf.at[:, pl.ds(1, num_ty - 1)], v_sems.at[2])
     took(bup.at[:, pl.ds(0, (num_tx - 1) * bup_w)], b_sems.at[SEND])
     took(yt_hbm, y_sems.at[RECV])
     took(xt.at[pl.ds(0, (n_dev - 1) * piece_w)], y_sems.at[SEND])
@@ -789,7 +805,7 @@
                    jax.ShapeDtypeStruct((max(n_layers - 1, 1), num_tx, width, col_w), BF16)),
         in_specs=[hb] + [vm] * 10 + [hb] * 7,
         out_specs=(hb,) * 4,
-        scratch_shapes=[V((n_tok,), jnp.int32), V((width, n_row), BF16), V((n_vec, LANES), F32), V((n_vec, LANES), BF16), V((n_dev, n_vec, LANES), BF16),
+        scratch_shapes=[V((n_tok,), jnp.int32), V((width, n_row), BF16), V((n_vec, LANES), F32), V((n_vec, LANES), BF16), V((num_tx, num_ty, n_vec, LANES), BF16),
                         V((n_vec, width), F32), V((8, b_up.shape[1]), F32), V((8, ff), F32),
                         V((3, d_rows, loc_heads, head_w), BF16), V((n_layers, 3, d_rows, loc_w), BF16),
                         V((width, 3 * loc_w), BF16), V((width, ff), BF16), V((num_tx, ff, col_w), BF16),
@@ -801,7 +817,7 @@
                         V((n_q, blk, head_w), BF16), V((n_row, width), BF16), V((n_chip, blk, ff), BF16),
                         V((n_chip, blk, width), F32), V((n_chip, n_row, width), F32),
                         V((2, n_row // 2, width), F32), V((4, n_row // 2, width), F32),
-                        ends, ends, ends, ends, dma((2, RG)), dma((2, RG)), dma((2, 3 * CG)),
+                        ends, dma((4,)), ends, ends, dma((2, RG)), dma((2, RG)), dma((2, 3 * CG)),
                         dma((n_layers, 2, CG)), dma((n_layers, 2, RG)), dma((2, 2 * CG)), dma((2, CG)), dma((6,)), ends, dma((2, 2 * n_chip * num_tx)),
                         dma((2, 12 * num_tx)), dma((4,)), ends],
         compiler_params=pltpu.CompilerParams(collective_id=1, has_side_effects=True, vmem_limit_bytes=63 << 20),

time: 304 us -> 298 us (0.980)
  Pallas kernels: 303 us -> 297 us
    pallas_call x1, Pallas kernels: 301 us -> 294 us  [decoder(): pl.pallas_call(functools.partial(decoder_kernel, num_tx, num_ty, n_layers...]
where the time goes in v3:
time: 298 us
  Pallas kernels  297 us (100%)
    pallas_call x1, Pallas kernels, decoder(): pl.pallas_call(functools.partial(decoder_kernel, num_tx, num_ty, n_layers...  294 us

profile of v3, /device:TPU:97, one launch (start us, length us, event | category | flops | bytes accessed | tf_op | source)
XLA Modules:
  0.0 297.6 jit_solution(13159028349358582676)
XLA Ops:
  0.6 294.2 %decoder.1 = (bf16[64,4096]{1,0:T(8,128)(2,1)}, bf16[2,1024,2,128]{3,2,1,0:T(2,128)(2,1)}, bf16[2,1024,2,128]{3,2,1,0:T(2,128)(2,1)}, bf16[1,4,2048,512]{3,2,1,0:T(8,128)(2,1)}) custom-call(bf16[64,4096]{1,0:T(8,128)(2,1)} %bitcast.3, bf16[2,64]{1,0:T(2,128)(2,1)} %g1_ref.1, bf16[2,64]{1,0:T(2,128)(2,1)} %b1_ref.1, bf16[2,64]{1,0:T(2,128)(2,1)} %g2_ref.1, ...), custom_call_target="tpu_custom_call" | custom-call | tf_op jit(solution)/shard_map/decoder/pallas_call | solution.py:802
  294.8 2.6 hand_over.1

commit v4 on v3

--- a/solution.py
+++ b/solution.py
@@ -31,6 +31,12 @@
 
 def rows(at, n):
     return pl.ds(pl.multiple_of(at, n), n)
+
+
+def unrolled_loop(n_from, n_to, body, value):
+    for n in range(n_from, n_to):
+        value = body(n, value)
+    return value
 
 
 class Place:
@@ -393,13 +399,20 @@
     def order(n):
         return n + n // 2 - 2 * (n // 3)
 
-    def each(n_from, n_to, body, hooks):
-        def step(n, carry):
-            for at_n, hook in hooks.items():
+    def at_step(n, hooks):
+        for at_n, hook in hooks.items():
+            if isinstance(n, int):
+                for h in hook if n == at_n else ():
+                    h()
+            else:
                 @pl.when(n == at_n)
                 def _():
                     for h in hook:
                         h()
+
+    def each(n_from, n_to, body, hooks):
+        def step(n, carry):
+            at_step(n, hooks)
             body(order(n))
             return carry
         lax.fori_loop(n_from, n_to, step, 0)
@@ -439,8 +452,9 @@
     n_grp = n_q * blk // q_grp
     n_sub = BK // blk
 
-    def attend(hooks):
+    def attend(hooks, unrolled):
         def step(n, carry):
+            loop = unrolled_loop if isinstance(n, int) else lax.fori_loop
             grp = n_grp - 1 - n
             q = qh[rows(grp * q_grp, q_grp), :]
             q_col = lax.broadcasted_iota(jnp.int32, (1, blk), 1)
@@ -461,7 +475,7 @@
                     full[j, :, i * q_grp:(i + 1) * q_grp] = part
                     m = jnp.maximum(m, jnp.max(part.reshape(blk // 8, 8, q_grp), axis=0))
                 return m
-            m = lax.fori_loop(0, grp, lambda j, m: score(j, m, False), jnp.full((8, q_grp), -1e30, F32))
+            m = loop(0, grp, lambda j, m: score(j, m, False), jnp.full((8, q_grp), -1e30, F32))
             m = jnp.max(score(grp, m, True), axis=0, keepdims=True)
 
             def expo(j, t):
@@ -470,13 +484,13 @@
                     full[j, :, i * q_grp:(i + 1) * q_grp] = e
                     t = t + jnp.sum(e.reshape(blk // 8, 8, q_grp), axis=0)
                 return t
-            t = lax.fori_loop(0, grp + 1, expo, jnp.zeros((8, q_grp), F32))
+            t = loop(0, grp + 1, expo, jnp.zeros((8, q_grp), F32))
             inv = 1.0 / jnp.sum(t, axis=0, keepdims=True)
 
             def apply(j, acc):
                 prob = jnp.concatenate([(full[j, :, i * q_grp:(i + 1) * q_grp] * inv).astype(BF16) for i in range(n_sub)], axis=0)
                 return acc + jnp.dot(vt[:, rows(j * BK, BK)], prob, preferred_element_type=F32)
-            out = lax.fori_loop(0, grp + 1, apply, jnp.zeros((head_w, q_grp), F32)).T.astype(BF16)
+            out = loop(0, grp + 1, apply, jnp.zeros((head_w, q_grp), F32)).T.astype(BF16)
             cols_o = rows((x * num_tx + y) * head_w, head_w)
             for i, b in enumerate(at_q):
                 ob[2 * grp + i] = out[i * blk:(i + 1) * blk]
@@ -485,13 +499,11 @@
                     here = jnp.logical_and(jnp.logical_and(yt == y, xd == x), c == r)
                     copy_or_send(here, ob.at[2 * grp + i, pl.ds(r * n_row, n_row)], obuf.at[:, cols_o], o_sems.at[SEND],
                                  o_sems.at[RECV], p.at(yt, xd * 2 + r))
-            for at_n, hook in hooks.items():
-                @pl.when(n == at_n)
-                def _():
-                    for h in hook:
-                        h()
+            at_step(n, hooks)
             return carry
-        lax.fori_loop(0, n_grp, step, 0)
+        if unrolled:
+            step(0, 0)
+        lax.fori_loop(1 if unrolled else 0, n_grp, step, 0)
 
     def up(l, k, n):
         half = wu.shape[1] // 2
@@ -652,7 +664,7 @@
             for k in (0, 1, last):
                 for ld in by_chip[k:k + 1]:
                     ld.start()
-        attend({0: [s_o[l].near], 1: [near_o, s_o[l].far]})
+        attend({0: [s_o[l].near], 1: [near_o, s_o[l].far]}, not first_layer)
         g_up[l].relay([0])
         g_up[l].start_second()
         g_up[l].relay([1])

time: 298 us -> 298 us (level)
  no operation moved by 1% of the time
where the time goes in v4:
time: 298 us
  Pallas kernels  297 us (100%)
    pallas_call x1, Pallas kernels, decoder(): pl.pallas_call(functools.partial(decoder_kernel, num_tx, num_ty, n_layers...  294 us

profile of v4, /device:TPU:97, one launch (start us, length us, event | category | flops | bytes accessed | tf_op | source)
XLA Modules:
  0.0 297.7 jit_solution(15341147799506251786)
XLA Ops:
  0.6 294.2 %decoder.1 = (bf16[64,4096]{1,0:T(8,128)(2,1)}, bf16[2,1024,2,128]{3,2,1,0:T(2,128)(2,1)}, bf16[2,1024,2,128]{3,2,1,0:T(2,128)(2,1)}, bf16[1,4,2048,512]{3,2,1,0:T(8,128)(2,1)}) custom-call(bf16[64,4096]{1,0:T(8,128)(2,1)} %bitcast.3, bf16[2,64]{1,0:T(2,128)(2,1)} %g1_ref.1, bf16[2,64]{1,0:T(2,128)(2,1)} %b1_ref.1, bf16[2,64]{1,0:T(2,128)(2,1)} %g2_ref.1, ...), custom_call_target="tpu_custom_call" | custom-call | tf_op jit(solution)/shard_map/decoder/pallas_call | solution.py:814
  294.8 2.6 hand_over.1
